TPU v7x, 256 devices: a whole 4x4x8 slice. The times are simulated.
256 devices in a mesh: grp: 8 (over y_hi, x), frag: 32 (over y_lo, z, core).
Axes of the slice: x: 4, y: 4 (y_hi: 2, y_lo: 2; y = y_hi * 2 + y_lo), z: 8, core: 2. Of those that a mesh axis runs over, the one named last changes fastest.
Arguments:
- density: bfloat16 [256, 9216], P('frag'), may hold values from -0.1 to 1, as said below
- fock_blocks: bfloat16 [256, 9216], P('frag'), may hold values from -8 to 8, as said below
- coupling: bfloat16 [1024, 9216], P(('grp', 'frag')), may hold values from -1.796875 to 1.796875
- dimer_pairs: int32 [1024, 2], P(('grp', 'frag')), may hold values from 0 to 255, as said below
- atom_counts: int32 [256], P('frag'), may hold values from 8 to 16
- nuclear_charge: float32 [4096], P('frag'), may hold values from 4 to 12
- coords: float32 [3, 4096], P(None, 'frag'), may hold values from -120 to 120
Outputs:
- density_correction: float32 [256, 9216], P('frag')
- dimer_energy: float32 [1024], P(('grp', 'frag'))
- total_energy: float32 [], replicated
Inputs may be any that keep to these rules, and one draw needn't show every extreme that they name: `dimer_pairs`: dimer d has fragments I < J; I // 8 == (d // 4) % 32, and J // 8 lies between I // 8 and I // 8 + 3. `density`: each row is a symmetric matrix. `fock_blocks`: each row is a symmetric matrix.
All inputs are finite; a program needn't handle non-finite values. Where the computation divides by a largest or mean magnitude, that divisor is 1e-20 or more.
Results may differ from a plain program's by a relative error of at most 0.0018.
Values may be sent and summed in bfloat16 or wider, within the bound.
No kernel may reach another device: no remote copies, remote signals or barrier semaphores. Data moves between devices by JAX's collectives and lax.ppermute only.
A program may use at most 64 MiB of HBM per device.

v0:
```python
import jax
import jax.numpy as jnp
from jax import lax
from jax.sharding import Mesh
from jax.sharding import PartitionSpec as P

NB = 96
NA = 16
REACH = 3
PURIF = 12
FRAG = ("frag_0", "frag_1", "frag_2")
GRP = ("grp_0", "grp_1")
GRP_FRAG = ("grp_0", "grp_1", "frag_0", "frag_1", "frag_2")


FULL_PRECISION = lax.Precision.HIGHEST


def from_everyone(value, axis):
    copies = jnp.broadcast_to(value, (lax.axis_size(axis), *value.shape))
    return lax.all_to_all(copies, axis, split_axis=0, concat_axis=0, tiled=True)


def joined_along(pieces, dim):
    shape = list(pieces.shape[1:])
    shape[dim] *= pieces.shape[0]
    return jnp.moveaxis(pieces, 0, dim).reshape(shape)


def collect(value, axis, dim):
    pieces = from_everyone(value, axis)
    return joined_along(pieces, dim)


def from_behind(value, axis, steps):
    count = lax.axis_size(axis)
    first, last = (max(0, -steps), min(count, count - steps))
    return lax.ppermute(value, axis, [(source, source + steps) for source in range(first, last)])


def in_blocks(value, dim, peers):
    shape = value.shape
    pieces = value.reshape(*shape[:dim], peers, shape[dim] // peers, *shape[dim + 1 :])
    return jnp.moveaxis(pieces, dim, 0)


def sent_and_summed(value, axis, dim):
    pieces = in_blocks(value, dim, lax.axis_size(axis))
    arrived = lax.all_to_all(pieces, axis, split_axis=0, concat_axis=0, tiled=True)
    return arrived.sum(axis=0)


def by_axis(value, axes):
    for axis in axes:
        value = lax.psum(value, axis)
    return value


def basis_atoms(count_real):
    basis_index = jnp.arange(NB, dtype=jnp.float32)[None, :, None]
    atom_index = jnp.arange(NA, dtype=jnp.float32)[None, None, :]
    scaled = basis_index * count_real[:, None, None]
    inside = jnp.logical_and(atom_index * NB <= scaled, scaled < (atom_index + 1.0) * NB)
    return inside.astype(jnp.float32)


def atom_table(density, nuclear_charge, atom_counts, coords):
    frag_count = density.shape[0]
    count_real = atom_counts.astype(jnp.float32)
    owners = basis_atoms(count_real)
    blocks = density.reshape(frag_count, NB, NB).astype(jnp.float32)
    on_diagonal = jnp.diagonal(blocks, axis1=1, axis2=2)
    population = 2.0 * jnp.sum(on_diagonal[:, :, None] * owners, axis=1)
    is_live = (jnp.arange(NA, dtype=jnp.float32)[None, :] < count_real[:, None]).astype(jnp.float32)
    charge = is_live * nuclear_charge.reshape(frag_count, NA) - population
    return jnp.concatenate([charge.reshape(1, -1), coords, is_live.reshape(1, -1)], axis=0)


def embed_potential(receivers, pair_ids, atom_rows):
    source_frag = jnp.arange(atom_rows.shape[1], dtype=jnp.int32) // NA
    keep_mask = jnp.logical_and(source_frag != pair_ids[0], source_frag != pair_ids[1]).astype(
        jnp.float32
    )
    offsets = receivers[1:4, :, None] - atom_rows[1:4, None, :]
    distance_sq = jnp.sum(offsets * offsets, axis=0)
    return jnp.sum((keep_mask * atom_rows[0])[None, :] / jnp.sqrt(distance_sq + 1.0), axis=1)


def dimer_solve(dens_pair, fock_pair, coupling_row, potential, count_pair):
    owners = basis_atoms(count_pair)
    site_shift = jnp.sum(owners * potential.reshape(2, 1, NA), axis=2)
    dens_blocks = dens_pair.astype(jnp.float32).reshape(2, NB, NB)
    fock_parts = fock_pair.astype(jnp.float32).reshape(2, NB, NB)
    cross_block = coupling_row.astype(jnp.float32).reshape(NB, NB)
    small_eye = jnp.eye(NB, dtype=jnp.float32)
    top_rows = jnp.concatenate(
        [fock_parts[0] + small_eye * site_shift[0][None, :], cross_block], axis=1
    )
    low_rows = jnp.concatenate(
        [cross_block.T, fock_parts[1] + small_eye * site_shift[1][None, :]], axis=1
    )
    dimer_fock = jnp.concatenate([top_rows, low_rows], axis=0)
    identity = jnp.eye(2 * NB, dtype=jnp.float32)
    centre = jnp.trace(dimer_fock) / (2.0 * NB)
    shifted = dimer_fock - centre * identity
    width = jnp.max(jnp.sum(jnp.abs(shifted), axis=1)) + 1e-06
    start = 0.5 * identity - shifted / (2.0 * width)

    def purify(index, current):
        square = jnp.dot(current, current, precision=FULL_PRECISION)
        return 3.0 * square - 2.0 * jnp.dot(square, current, precision=FULL_PRECISION)

    purified = lax.fori_loop(0, PURIF, purify, start)
    zero_block = jnp.zeros((NB, NB), jnp.float32)
    start_guess = jnp.concatenate(
        [
            jnp.concatenate([dens_blocks[0], zero_block], axis=1),
            jnp.concatenate([zero_block, dens_blocks[1]], axis=1),
        ],
        axis=0,
    )
    energy = jnp.sum((purified - start_guess) * dimer_fock.T)
    changes = jnp.stack([purified[:NB, :NB] - dens_blocks[0], purified[NB:, NB:] - dens_blocks[1]])
    return (changes.reshape(2, NB * NB), energy)


def per_device(density, fock_blocks, coupling, dimer_pairs, atom_counts, nuclear_charge, coords):
    frag_dev = density.shape[0]
    local_rows = atom_table(density, nuclear_charge, atom_counts, coords)
    atom_rows = collect(local_rows, FRAG, 1)
    my_index = lax.axis_index(FRAG)
    dens_list = [density]
    fock_list = [fock_blocks]
    for distance in range(1, REACH + 1):
        got_dens, got_fock = from_behind((density, fock_blocks), FRAG, -distance)
        dens_list.append(got_dens)
        fock_list.append(got_fock)
    held_dens = jnp.concatenate(dens_list, axis=0)
    held_fock = jnp.concatenate(fock_list, axis=0)
    first_row = my_index * frag_dev
    held_index = dimer_pairs - first_row

    def solve_one(pair_ids, row_pair, coupling_row):
        columns = (pair_ids[:, None] * NA + jnp.arange(NA, dtype=jnp.int32)[None, :]).reshape(-1)
        receivers = jnp.take(atom_rows, columns, axis=1)
        potential = embed_potential(receivers, pair_ids, atom_rows)
        count_pair = jnp.sum(receivers[4].reshape(2, NA), axis=1)
        return dimer_solve(
            jnp.take(held_dens, row_pair, axis=0),
            jnp.take(held_fock, row_pair, axis=0),
            coupling_row,
            potential,
            count_pair,
        )

    changes, energies = jax.vmap(solve_one)(dimer_pairs, held_index, coupling)
    held_count = held_dens.shape[0]
    selector = (
        jnp.arange(held_count, dtype=jnp.int32)[:, None] == held_index.reshape(1, -1)
    ).astype(jnp.float32)
    partial_value = jnp.dot(selector, changes.reshape(-1, NB * NB), precision=FULL_PRECISION)
    partial_value = sent_and_summed(partial_value, GRP, 1)
    own_rows = partial_value[:frag_dev]
    for distance in range(1, REACH + 1):
        piece = partial_value[distance * frag_dev : (distance + 1) * frag_dev]
        own_rows = own_rows + from_behind(piece.astype(jnp.bfloat16), FRAG, distance).astype(
            piece.dtype
        )
    own_rows = collect(own_rows, GRP, 1)
    total_energy = by_axis(jnp.sum(energies), GRP_FRAG)
    return (own_rows, energies, total_energy)


def solution(mesh):
    finer = Mesh(
        mesh.devices.reshape(2, 4, 2, 8, 2), ("grp_0", "grp_1", "frag_0", "frag_1", "frag_2")
    )
    return jax.shard_map(
        per_device,
        mesh=finer,
        in_specs=(
            P(FRAG, None),
            P(FRAG, None),
            P(GRP_FRAG, None),
            P(GRP_FRAG, None),
            P(FRAG),
            P(FRAG),
            P(None, FRAG),
        ),
        out_specs=(P(FRAG, None), P(GRP_FRAG), P()),
        check_vma=False,
    )
```

profile of v0, /device:TPU:1, one launch (start us, length us, event | category | flops | bytes accessed | tf_op | source)
XLA Modules:
  0.0 172.8 jit_solution(6586813165077546668)
XLA Ops:
  0.6 5.1 %collective-permute-start = (bf16[8,9216]{1,0:T(8,128)(2,1)}, bf16[8,9216]{1,0:T(8,128)(2,1)S(1)}, u32[]{:S(2)}, u32[]{:S(2)}) collective-permute-start(bf16[8,9216]{1,0:T(8,128)(2,1)} %param.12), channel_id=1, source_target_pairs={{1,0},{2,1},{3,2},{4,3},{5,4},{6,5},{7,6},{8,7},{9,8},{10,9},{11,1... | collective-permute-start | bytes 442376 | tf_op jit(solution)/shard_map/ppermute | solution.py:38
  5.7 1.3 collective-permute-start.1
  7.0 1.3 collective-permute-start.2
  8.3 1.9 %collective-permute-start.3 = (bf16[8,9216]{1,0:T(8,128)(2,1)}, bf16[8,9216]{1,0:T(8,128)(2,1)S(1)}, u32[]{:S(2)}, u32[]{:S(2)}) collective-permute-start(bf16[8,9216]{1,0:T(8,128)(2,1)} %param.11), channel_id=1, source_target_pairs={{1,0},{2,1},{3,2},{4,3},{5,4},{6,5},{7,6},{8,7},{9,8},{10,9},{11,1... | collective-permute-start | bytes 442376 | tf_op jit(solution)/shard_map/ppermute | solution.py:38
  10.3 1.3 collective-permute-start.4
  11.7 3.4 %copy.86 = f32[8,9216]{0,1:T(8,128)} copy(bf16[8,9216]{1,0:T(8,128)(2,1)} %param.11) | data formatting | bytes 442368 | tf_op jit(solution)/shard_map/convert_element_type | solution.py:71
  15.3 2.9 %gather_fusion = f32[96,8]{1,0:T(8,128)S(1)} fusion(f32[8,96,96]{0,2,1:T(8,128)} %bitcast.84, s32[96]{0:T(128)S(1)} %or_bitcast_fusion), kind=kCustom, calls=%fused_computation.2 | custom fusion | bytes 6912 | tf_op jit(solution)/shard_map/jit(diagonal)/gather | solution.py:72
  19.4 15.1 %all-to-all-start = ((f32[32,5,128]{2,1,0:T(8,128)}), f32[32,5,128]{2,1,0:T(8,128)S(1)}, u32[]{:S(2)}, u32[]{:S(2)}) async-start(f32[32,5,128]{2,1,0:T(8,128)} %broadcast_in_dim.37), calls=%async_computation | async-start | bytes 262144 | tf_op jit(solution)/shard_map/all_to_all | solution.py:21
  40.1 1.3 collective-permute-start.5
  42.2 8.3 %collective-permute-done.5 = bf16[8,9216]{1,0:T(8,128)(2,1)S(1)} collective-permute-done((bf16[8,9216]{1,0:T(8,128)(2,1)S(1)}, bf16[8,9216]{1,0:T(8,128)(2,1)S(1)}, u32[]{:S(2)}, u32[]{:S(2)}) %collective-permute-start.5) | collective-permute-done | bytes 147488 | tf_op jit(solution)/shard_map/ppermute | solution.py:38
  53.7 1.5 copy.89
  60.9 23.0 %while.10 = (s32[]{:T(128)}, f32[4,192,192]{2,1,0:T(8,128)S(1)}, s32[]{:T(128)}) while((s32[]{:T(128)}, f32[4,192,192]{2,1,0:T(8,128)S(1)}, s32[]{:T(128)}) %tuple.36), condition=%wide.region_9.11_spmd, body=%wide.region_8.10_spmd.sunk | while | flops 679919616 | bytes 4128813 | solution.py:113
  61.9 0.9 fusion.42
  63.8 0.9 fusion.42
  65.7 0.9 fusion.42
  67.6 0.9 fusion.42
  69.5 0.9 fusion.42
  71.5 0.9 fusion.42
  73.4 0.9 fusion.42
  77.2 0.9 fusion.42
  81.0 0.9 fusion.42
  85.8 22.6 %all_to_all.15 = f32[8,32,1152]{2,1,0:T(8,128)S(1)} all-to-all(f32[8,32,1152]{2,1,0:T(8,128)S(1)} %convolution_bitcast_fusion), channel_id=1, replica_groups=mesh['grp_0'=2,'grp_1'=4,'frag_0'=2,'frag_1'=8,'frag_2'=2] {'grp_0','grp..., dimensions={0} | all-to-all | bytes 2359296 | tf_op jit(solution)/shard_map/all_to_all | solution.py:49
  108.5 5.4 %collective-permute-start.6 = (bf16[8,1152]{1,0:T(8,128)(2,1)S(1)}, bf16[8,1152]{1,0:T(8,128)(2,1)S(1)}, u32[]{:S(2)}, u32[]{:S(2)}) collective-permute-start(bf16[8,1152]{1,0:T(8,128)(2,1)S(1)} %get-tuple-element.33), channel_id=1, source_target_pairs={{0,1},{1,2},{2,3},{3,4},{4,5},{5,6},{6,7},{7,8},{8,9},{9,10},{10,1... | collective-permute-start | bytes 55304 | tf_op jit(solution)/shard_map/ppermute | solution.py:38
  113.8 1.3 collective-permute-start.7
  115.1 6.0 %collective-permute-start.8 = (bf16[8,1152]{1,0:T(8,128)(2,1)S(1)}, bf16[8,1152]{1,0:T(8,128)(2,1)S(1)}, u32[]{:S(2)}, u32[]{:S(2)}) collective-permute-start(bf16[8,1152]{1,0:T(8,128)(2,1)S(1)} %get-tuple-element.34), channel_id=1, source_target_pairs={{0,3},{1,4},{2,5},{3,6},{4,7},{5,8},{6,9},{7,10},{8,11},{9,12},{10... | collective-permute-start | bytes 55304 | tf_op jit(solution)/shard_map/ppermute | solution.py:38
  122.7 3.4 %all-to-all-start.2 = ((f32[8,8,1152]{2,1,0:T(8,128)}), f32[8,8,1152]{2,1,0:T(8,128)S(1)}, u32[]{:S(2)}, u32[]{:S(2)}) async-start(f32[8,8,1152]{2,1,0:T(8,128)} %broadcast_in_dim.44), calls=%async_computation.2 | async-start | bytes 589824 | tf_op jit(solution)/shard_map/all_to_all | solution.py:21
  126.2 1.0 fusion.21
  127.1 6.0 %psum.35 = f32[]{:T(128)} all-reduce(f32[]{:T(128)} %get-tuple-element.19), channel_id=1, replica_groups=mesh['grp_0'=2,'grp_1'=4,'frag_0'=2,'frag_1'=8,'frag_2'=2] {'grp_0'}, use_global_device_ids=true, to_apply=%region_13.15 | all-reduce | flops 1 | bytes 8 | tf_op jit(solution)/shard_map/psum | solution.py:55
  133.1 9.5 %psum.36 = f32[]{:T(128)} all-reduce(f32[]{:T(128)} %psum.35), channel_id=1, replica_groups=mesh['grp_0'=2,'grp_1'=4,'frag_0'=2,'frag_1'=8,'frag_2'=2] {'grp_1'}, use_global_device_ids=true, to_apply=%region_14.16 | all-reduce | flops 1 | bytes 8 | tf_op jit(solution)/shard_map/psum | solution.py:55
  142.6 4.8 %psum.37 = f32[]{:T(128)} all-reduce(f32[]{:T(128)} %psum.36), channel_id=1, replica_groups=mesh['grp_0'=2,'grp_1'=4,'frag_0'=2,'frag_1'=8,'frag_2'=2] {'frag_0'}, use_global_device_ids=true, to_apply=%region_15.17 | all-reduce | flops 1 | bytes 8 | tf_op jit(solution)/shard_map/psum | solution.py:55
  147.4 13.6 %psum.38 = f32[]{:T(128)} all-reduce(f32[]{:T(128)} %psum.37), channel_id=1, replica_groups=mesh['grp_0'=2,'grp_1'=4,'frag_0'=2,'frag_1'=8,'frag_2'=2] {'frag_1'}, use_global_device_ids=true, to_apply=%region_16.18 | all-reduce | flops 1 | bytes 8 | tf_op jit(solution)/shard_map/psum | solution.py:55
  160.9 11.1 %psum.39 = f32[]{:T(128)} all-reduce(f32[]{:T(128)} %psum.38), channel_id=1, replica_groups=mesh['grp_0'=2,'grp_1'=4,'frag_0'=2,'frag_1'=8,'frag_2'=2] {'frag_2'}, use_global_device_ids=true, to_apply=%region_17.19 | all-reduce | flops 1 | bytes 8 | tf_op jit(solution)/shard_map/psum | solution.py:55
  (166 shorter events, 34.6 us)
Async XLA Ops:
  0.6 39.4 %collective-permute-start = (bf16[8,9216]{1,0:T(8,128)(2,1)}, bf16[8,9216]{1,0:T(8,128)(2,1)S(1)}, u32[]{:S(2)}, u32[]{:S(2)}) collective-permute-start(bf16[8,9216]{1,0:T(8,128)(2,1)} %param.12), channel_id=1, source_target_pairs={{1,0},{2,1},{3,2},{4,3},{5,4},{6,5},{7,6},{8,7},{9,8},{10,9},{11,1... | collective-permute-start | bytes 442376 | tf_op jit(solution)/shard_map/ppermute | solution.py:38
  5.7 35.6 %collective-permute-start.1 = (bf16[8,9216]{1,0:T(8,128)(2,1)}, bf16[8,9216]{1,0:T(8,128)(2,1)S(1)}, u32[]{:S(2)}, u32[]{:S(2)}) collective-permute-start(bf16[8,9216]{1,0:T(8,128)(2,1)} %param.12), channel_id=1, source_target_pairs={{2,0},{3,1},{4,2},{5,3},{6,4},{7,5},{8,6},{9,7},{10,8},{11,9},{12,... | collective-permute-start | bytes 442376 | tf_op jit(solution)/shard_map/ppermute | solution.py:38
  7.0 34.3 %collective-permute-start.2 = (bf16[8,9216]{1,0:T(8,128)(2,1)}, bf16[8,9216]{1,0:T(8,128)(2,1)S(1)}, u32[]{:S(2)}, u32[]{:S(2)}) collective-permute-start(bf16[8,9216]{1,0:T(8,128)(2,1)} %param.12), channel_id=1, source_target_pairs={{3,0},{4,1},{5,2},{6,3},{7,4},{8,5},{9,6},{10,7},{11,8},{12,9},{13... | collective-permute-start | bytes 442376 | tf_op jit(solution)/shard_map/ppermute | solution.py:38
  8.3 33.8 %collective-permute-start.3 = (bf16[8,9216]{1,0:T(8,128)(2,1)}, bf16[8,9216]{1,0:T(8,128)(2,1)S(1)}, u32[]{:S(2)}, u32[]{:S(2)}) collective-permute-start(bf16[8,9216]{1,0:T(8,128)(2,1)} %param.11), channel_id=1, source_target_pairs={{1,0},{2,1},{3,2},{4,3},{5,4},{6,5},{7,6},{8,7},{9,8},{10,9},{11,1... | collective-permute-start | bytes 442376 | tf_op jit(solution)/shard_map/ppermute | solution.py:38
  10.3 31.9 %collective-permute-start.4 = (bf16[8,9216]{1,0:T(8,128)(2,1)}, bf16[8,9216]{1,0:T(8,128)(2,1)S(1)}, u32[]{:S(2)}, u32[]{:S(2)}) collective-permute-start(bf16[8,9216]{1,0:T(8,128)(2,1)} %param.11), channel_id=1, source_target_pairs={{2,0},{3,1},{4,2},{5,3},{6,4},{7,5},{8,6},{9,7},{10,8},{11,9},{12,... | collective-permute-start | bytes 442376 | tf_op jit(solution)/shard_map/ppermute | solution.py:38
  11.6 6.7 %copy-start.13 = (f32[16]{0:T(128)}, f32[16]{0:T(128)S(1)}, u32[]{:S(2)}) copy-start(f32[16]{0:T(128)S(1)} %get-tuple-element.44) | copy-start | bytes 196
  11.6 6.7 %copy-start.15 = (f32[16]{0:T(128)}, f32[16]{0:T(128)S(1)}, u32[]{:S(2)}) copy-start(f32[16]{0:T(128)S(1)} %get-tuple-element.45) | copy-start | bytes 196
  11.6 3.5 %copy-start.18 = (s32[8]{0:T(128)S(1)}, s32[8]{0:T(128)}, u32[]{:S(2)}) copy-start(s32[8]{0:T(128)} %param.15) | copy-start | bytes 100
  11.6 7.1 %copy-start.17 = (f32[128]{0:T(128)S(1)}, f32[128]{0:T(128)}, u32[]{:S(2)}) copy-start(f32[128]{0:T(128)} %param.16) | copy-start | bytes 1540
  11.6 7.1 %copy-start.12 = (f32[3,128]{1,0:T(4,128)S(1)}, f32[3,128]{1,0:T(4,128)}, u32[]{:S(2)}) copy-start(f32[3,128]{1,0:T(4,128)} %param.17) | copy-start | bytes 4612
  11.6 22.9 %copy-start.8 = (s32[4,2]{0,1:T(2,128)S(1)}, s32[4,2]{0,1:T(2,128)}, u32[]{:S(2)}) copy-start(s32[4,2]{0,1:T(2,128)} %param.14) | copy-start | bytes 100
  11.7 26.8 %copy-start.6 = (bf16[4,9216]{1,0:T(4,128)(2,1)S(1)}, bf16[4,9216]{1,0:T(4,128)(2,1)}, u32[]{:S(2)}) copy-start(bf16[4,9216]{1,0:T(4,128)(2,1)} %param.13) | copy-start | bytes 221188
  15.1 25.0 %copy-start.2 = (bf16[8,9216]{1,0:T(8,128)(2,1)S(1)}, bf16[8,9216]{1,0:T(8,128)(2,1)}, u32[]{:S(2)}) copy-start(bf16[8,9216]{1,0:T(8,128)(2,1)} %param.11) | copy-start | bytes 442372
  15.1 26.3 %copy-start.5 = (bf16[8,9216]{1,0:T(8,128)(2,1)S(1)}, bf16[8,9216]{1,0:T(8,128)(2,1)}, u32[]{:S(2)}) copy-start(bf16[8,9216]{1,0:T(8,128)(2,1)} %param.12) | copy-start | bytes 442372
  19.4 33.0 %all-to-all-start = ((f32[32,5,128]{2,1,0:T(8,128)}), f32[32,5,128]{2,1,0:T(8,128)S(1)}, u32[]{:S(2)}, u32[]{:S(2)}) async-start(f32[32,5,128]{2,1,0:T(8,128)} %broadcast_in_dim.37), calls=%async_computation | async-start | bytes 262144 | tf_op jit(solution)/shard_map/all_to_all | solution.py:21
  40.1 10.4 %collective-permute-start.5 = (bf16[8,9216]{1,0:T(8,128)(2,1)S(1)}, bf16[8,9216]{1,0:T(8,128)(2,1)S(1)}, u32[]{:S(2)}, u32[]{:S(2)}) collective-permute-start(bf16[8,9216]{1,0:T(8,128)(2,1)S(1)} %copy-done.2), channel_id=1, source_target_pairs={{3,0},{4,1},{5,2},{6,3},{7,4},{8,5},{9,6},{10,7},{11,8},{12,9},{13... | collective-permute-start | bytes 442376 | tf_op jit(solution)/shard_map/ppermute | solution.py:38
  52.4 1.3 copy-start
  56.1 2.4 %copy-start.7 = (f32[4096]{0:T(1024)S(1)}, f32[4096]{0:T(1024)}, u32[]{:S(2)}) copy-start(f32[4096]{0:T(1024)} %slice_bitcast_fusion.3) | copy-start | bytes 49156
  56.1 2.4 %copy-start.10 = (s32[4]{0:T(128)S(1)}, s32[4]{0:T(128)}, u32[]{:S(2)}) copy-start(s32[4]{0:T(128)} %get-tuple-element.38) | copy-start | bytes 52
  56.1 2.4 %copy-start.11 = (s32[4]{0:T(128)S(1)}, s32[4]{0:T(128)}, u32[]{:S(2)}) copy-start(s32[4]{0:T(128)} %get-tuple-element.39) | copy-start | bytes 52
  58.4 0.9 copy-start.14
  58.4 0.9 copy-start.16
  58.4 1.0 copy-start.4
  58.6 1.0 copy-start.3
  59.5 1.1 copy-start.1
  84.3 0.7 copy-start.9
  108.5 12.6 %collective-permute-start.6 = (bf16[8,1152]{1,0:T(8,128)(2,1)S(1)}, bf16[8,1152]{1,0:T(8,128)(2,1)S(1)}, u32[]{:S(2)}, u32[]{:S(2)}) collective-permute-start(bf16[8,1152]{1,0:T(8,128)(2,1)S(1)} %get-tuple-element.33), channel_id=1, source_target_pairs={{0,1},{1,2},{2,3},{3,4},{4,5},{5,6},{6,7},{7,8},{8,9},{9,10},{10,1... | collective-permute-start | bytes 55304 | tf_op jit(solution)/shard_map/ppermute | solution.py:38
  113.8 7.3 %collective-permute-start.7 = (bf16[8,1152]{1,0:T(8,128)(2,1)S(1)}, bf16[8,1152]{1,0:T(8,128)(2,1)S(1)}, u32[]{:S(2)}, u32[]{:S(2)}) collective-permute-start(bf16[8,1152]{1,0:T(8,128)(2,1)S(1)} %get-tuple-element.35), channel_id=1, source_target_pairs={{0,2},{1,3},{2,4},{3,5},{4,6},{5,7},{6,8},{7,9},{8,10},{9,11},{10,... | collective-permute-start | bytes 55304 | tf_op jit(solution)/shard_map/ppermute | solution.py:38
  115.1 6.8 %collective-permute-start.8 = (bf16[8,1152]{1,0:T(8,128)(2,1)S(1)}, bf16[8,1152]{1,0:T(8,128)(2,1)S(1)}, u32[]{:S(2)}, u32[]{:S(2)}) collective-permute-start(bf16[8,1152]{1,0:T(8,128)(2,1)S(1)} %get-tuple-element.34), channel_id=1, source_target_pairs={{0,3},{1,4},{2,5},{3,6},{4,7},{5,8},{6,9},{7,10},{8,11},{9,12},{10... | collective-permute-start | bytes 55304 | tf_op jit(solution)/shard_map/ppermute | solution.py:38
  122.7 49.3 %all-to-all-start.2 = ((f32[8,8,1152]{2,1,0:T(8,128)}), f32[8,8,1152]{2,1,0:T(8,128)S(1)}, u32[]{:S(2)}, u32[]{:S(2)}) async-start(f32[8,8,1152]{2,1,0:T(8,128)} %broadcast_in_dim.44), calls=%async_computation.2 | async-start | bytes 589824 | tf_op jit(solution)/shard_map/all_to_all | solution.py:21
where the time goes:
time: 174 us; the launch traced here: 173 us
  blocking collectives  67.5 us (39%)
  starting transfers between devices  43.3 us (25%)
  matrix products  22.6 us (13%)
  local copies, waits for them, and re-layouts  19.7 us (11%)
  waiting for transfers between devices  9.16 us (5%)
  other arithmetic  8.75 us (5%)
    psum x5, blocking collectives, by_axis(): value = lax.psum(value, axis)  44.9 us
    ppermute x9, starting transfers between devices, from_behind(): lax.ppermute(value, axis, [(source, source + steps) for source in range(f...  24.8 us
    all_to_all x1, blocking collectives, sent_and_summed(): lax.all_to_all(pieces, axis, split_axis=0, concat_axis=0, tiled=True)  22.6 us
    all_to_all x2, starting transfers between devices, from_everyone(): return lax.all_to_all(copies, axis, split_axis=0, concat_axis=0, tiled=True)  18.5 us
    dot_general x12, matrix products, purify(): jnp.dot(square, current, precision=FULL_PRECISION)  11.2 us
    dot_general x12, matrix products, purify(): square = jnp.dot(current, current, precision=FULL_PRECISION)  10.7 us
    ppermute x9, waiting for transfers between devices, from_behind(): lax.ppermute(value, axis, [(source, source + steps) for source in range(f...  9.15 us
  transfers between devices with their start and end apart: 11, of which 2 were waited for; matrix products, arithmetic and copies ran while one was open for 10% of the time, Pallas kernels for 0%

commit v1 on v0

v1 whole, which is shorter than its diff:
```python
import jax
import jax.numpy as jnp
from jax import lax
from jax.experimental import pallas as pl
from jax.experimental.pallas import tpu as pltpu
from jax.sharding import Mesh
from jax.sharding import PartitionSpec as P

NB = 96
NA = 16
REACH = 3
PURIF = 12
FRAG_DEV = 8
DIM_DEV = 4
FLAT = NB * NB
FRAG = ("frag_0", "frag_1", "frag_2")
PAIR = ("frag_0", "frag_1")
GRP_FRAG = ("grp_0", "grp_1", "frag_0", "frag_1", "frag_2")
TEAM = ("grp_0", "grp_1", "frag_2")
N_FRAG = 32
N_PAIR = 16
N_TEAM = 16
N_GRP = 8
F32 = jnp.float32
BF16 = jnp.bfloat16
VMEM = pltpu.VMEM
SMEM = pltpu.SMEM

ID_LANE = 96
ONE_LANE = 97
ENERGY_LANE = 98
SUM_LANE = 99


def iota(shape, dim):
    return lax.broadcasted_iota(jnp.int32, shape, dim)


def exchange(value, axis):
    return lax.all_to_all(value, axis, split_axis=0, concat_axis=0, tiled=True)


def dot32(left, right):
    return jnp.dot(left, right, preferred_element_type=F32)


def halves(value):
    high = value.astype(BF16)
    return high, (value - high.astype(F32)).astype(BF16)


def table_kernel(counts, dens, fock, nuclear, coords, table):
    lane = iota((1, 128), 1)
    trace_sum = jnp.zeros((FRAG_DEV, 128), F32)
    diagonal = jnp.zeros((FRAG_DEV, 128), F32)
    for chunk in range(FLAT // 128):
        here = slice(chunk * 128, (chunk + 1) * 128)
        block = dens[:, here].astype(F32)
        trace_sum += block * fock[:, here].astype(F32)
        first = (-chunk * 128) % (NB + 1)
        on_diagonal = jnp.logical_or(lane == first, lane == first + NB + 1)
        diagonal += jnp.where(on_diagonal, block, 0.0)
    fragment = lane // NA
    atom = (lane % NA).astype(F32)
    count = jnp.zeros((1, 128), F32)
    for index in range(FRAG_DEV):
        count = jnp.where(fragment == index, counts[index].astype(F32), count)
    basis = (iota((128, 128), 0) * 33) % 128
    scaled = basis.astype(F32) * count
    inside = jnp.logical_and(atom * NB <= scaled, scaled < (atom + 1.0) * NB)
    owner = jnp.where(jnp.logical_and(inside, basis < NB), 1.0, 0.0).astype(BF16)
    spread = dot32(diagonal.astype(BF16), owner)
    own_lane = iota((FRAG_DEV, 128), 0) == fragment
    population = jnp.sum(jnp.where(own_lane, spread, 0.0), axis=0, keepdims=True)
    traces = jnp.sum(trace_sum, axis=1, keepdims=True)
    at_first = jnp.logical_and(own_lane, lane % NA == 0)
    trace_row = jnp.sum(jnp.where(at_first, traces, 0.0), axis=0, keepdims=True)
    live = jnp.where(atom < count, 1.0, 0.0)
    charge = live * nuclear[...] - 2.0 * population
    row = iota((8, 128), 0)
    rows = [charge, coords[0:1, :], coords[1:2, :], coords[2:3, :], count, population, trace_row]
    value = jnp.zeros((8, 128), F32)
    for index, content in enumerate(rows):
        value = jnp.where(row == index, content, value)
    for peer in range(N_FRAG):
        table[peer] = value


def atom_table(density, fock_blocks, nuclear_charge, atom_counts, coords):
    return pl.pallas_call(
        table_kernel,
        out_shape=jax.ShapeDtypeStruct((N_FRAG, 8, 128), F32),
        in_specs=[pl.BlockSpec(memory_space=SMEM)] + [pl.BlockSpec(memory_space=VMEM)] * 4,
        out_specs=pl.BlockSpec(memory_space=VMEM),
        name="atom_table",
    )(atom_counts, density, fock_blocks, nuclear_charge.reshape(1, 128), coords)


def solve_kernel(
    pairs, table, fock_0, fock_1, fock_2, fock_3, coupling, sent, energies,
    columns, masked, fock_j, shifted, state, high, low, square_high, square_low,
):
    focks = (fock_0, fock_1, fock_2, fock_3)
    base = (pairs[0] // FRAG_DEV) * FRAG_DEV
    pair_base = (base // NA) * NA
    lane = iota((NA, 128), 1)
    atom = iota((NA, 128), 0).astype(F32)

    shifted[...] = jnp.zeros_like(shifted)
    for buffer in (high, low, square_high, square_low):
        for dimer in range(DIM_DEV):
            buffer[dimer, NB:128, :] = jnp.zeros((128 - NB, 256), BF16)
            buffer[dimer, 128 + NB :, :] = jnp.zeros((128 - NB, 256), BF16)

    source = iota((N_FRAG, 128), 0) * FRAG_DEV + iota((N_FRAG, 128), 1) // NA
    charges = table[:, 0, :]
    for dimer in range(DIM_DEV):
        first, second = pairs[2 * dimer], pairs[2 * dimer + 1]
        hidden = jnp.logical_or(source == first, source == second)
        masked[dimer] = jnp.where(hidden, 0.0, charges)
        for side in range(2):
            fragment = pairs[2 * dimer + side]
            columns[2 * dimer + side] = table[fragment // FRAG_DEV].T

    shifts, starts = [], []
    for dimer in range(DIM_DEV):
        own, places = [], []
        for side in range(2):
            local = pl.multiple_of((pairs[2 * dimer + side] % FRAG_DEV) * NA, NA)
            mine = columns[2 * dimer + side, pl.ds(local, NA), :]
            own.append(mine)
            places.append([jnp.broadcast_to(mine[:, k : k + 1], (NA, 128)) for k in (1, 2, 3)])

        def gather(step, sums, dimer=dimer, places=places):
            sums = list(sums)
            for inner in range(4):
                block = step * 4 + inner
                weight = masked[dimer, pl.ds(block, 1), :]
                spot = [table[block, k : k + 1, :] for k in (1, 2, 3)]
                for side in range(2):
                    delta = [place - here for place, here in zip(places[side], spot)]
                    distance = delta[0] * delta[0] + delta[1] * delta[1] + delta[2] * delta[2]
                    sums[side] += weight * lax.rsqrt(distance + 1.0)
            return tuple(sums)

        zero = jnp.zeros((NA, 128), F32)
        sums = lax.fori_loop(0, N_FRAG // 4, gather, (zero, zero))
        start = jnp.zeros((1, 1), F32)
        for side in range(2):
            potential = jnp.sum(sums[side], axis=1, keepdims=True)
            count, population, trace = (own[side][:, k : k + 1] for k in (4, 5, 6))
            scaled = lane.astype(F32) * count
            inside = jnp.logical_and(atom * NB <= scaled, scaled < (atom + 1.0) * NB)
            inside = jnp.logical_and(inside, lane < NB)
            shifts.append(jnp.sum(jnp.where(inside, potential, 0.0), axis=0, keepdims=True))
            start += jnp.sum(potential * population + trace, axis=0, keepdims=True)
        starts.append(start)

    small_eye = iota((NB, NB), 0) == iota((NB, NB), 1)
    rows, cols = iota((2 * NB, 256), 0), iota((2 * NB, 256), 1)
    eye = cols == jnp.where(rows < NB, rows, rows + (128 - NB))
    centres, widths = [], []
    for dimer in range(DIM_DEV):
        second = pairs[2 * dimer + 1] - base
        for far in range(REACH + 1):

            @pl.when(second // FRAG_DEV == far)
            def _(far=far, second=second):
                fock_j[...] = focks[far][second % FRAG_DEV]

        cross = coupling[dimer].astype(F32)
        for side in range(2):
            at, to = side * NB, side * 128
            part = fock_0[pairs[2 * dimer] - base] if side == 0 else fock_j[...]
            shift = shifts[2 * dimer + side][:, :NB]
            shifted[dimer, at : at + NB, to : to + NB] = part.astype(F32) + jnp.where(
                small_eye, shift, 0.0
            )
        shifted[dimer, :NB, 128 : 128 + NB] = cross
        shifted[dimer, NB:, :NB] = cross.T
        fock = shifted[dimer]
        trace = jnp.sum(jnp.where(eye, fock, 0.0), axis=(0, 1), keepdims=True)
        centre = trace / (2.0 * NB)
        fock = jnp.where(eye, fock - centre, fock)
        width = jnp.max(jnp.sum(jnp.abs(fock), axis=1, keepdims=True), axis=0, keepdims=True) + 1e-06
        shifted[dimer] = fock
        start = fock / width
        state[dimer] = start
        keep(high, low, dimer, start)
        centres.append(centre)

    def purify(step, carry):
        for dimer in range(DIM_DEV):
            square = product(high, low, dimer, high, low)
            keep(square_high, square_low, dimer, square)
        for dimer in range(DIM_DEV):
            cube = product(high, low, dimer, square_high, square_low)
            later = 1.5 * state[dimer] - 0.5 * cube
            state[dimer] = later
            keep(high, low, dimer, later)
        return carry

    lax.fori_loop(0, PURIF, purify, 0)

    last = jnp.zeros((1, 128), F32)
    row_lane = iota((1, 128), 1)
    lane_16 = iota((16, 128), 1)
    for dimer in range(DIM_DEV):
        final = state[dimer]
        overlap = jnp.sum(final * shifted[dimer], axis=(0, 1), keepdims=True)
        trace = jnp.sum(jnp.where(eye, final, 0.0), axis=(0, 1), keepdims=True)
        centre = centres[dimer]
        energy = 0.5 * (2.0 * NB * centre - overlap - centre * trace) - starts[dimer]
        last = jnp.where(row_lane == dimer, energy, last)
        for side in range(2):
            slot = side * DIM_DEV + dimer
            block = final[side * NB : (side + 1) * NB, side * 128 : (side + 1) * 128]
            corner = pltpu.roll(block[64:96, :], 32, 1)
            target = (pairs[2 * dimer + side] - pair_base).astype(F32)
            beside = jnp.where(lane_16 == ID_LANE, target, 0.0)
            beside = jnp.where(lane_16 == ONE_LANE, 1.0, beside)
            if side == 0:
                beside = jnp.where(lane_16 == ENERGY_LANE, energy, beside)
            for part in range(4):
                piece = block[16 * part : 16 * (part + 1), :]
                other = corner[16 * part : 16 * (part + 1), :] if part < 2 else beside
                piece = jnp.where(lane_16 < NB, piece, other)
                sent[pl.ds(part * 8 + slot, 16, stride=32), :] = piece
    energies[...] = last


def keep(high, low, dimer, value):
    upper, lower = halves(value)
    for buffer, part in ((high, upper), (low, lower)):
        buffer[dimer, :NB, :] = part[:NB]
        buffer[dimer, 128 : 128 + NB, :] = part[NB:]


def product(high, low, dimer, right_high, right_low):
    upper = [high[dimer, :NB, :], high[dimer, 128 : 128 + NB, :]]
    lower = [low[dimer, :NB, :], low[dimer, 128 : 128 + NB, :]]
    both = dot32(jnp.concatenate(upper + lower, axis=0), right_high[dimer])
    cross = dot32(jnp.concatenate(upper, axis=0), right_low[dimer])
    return both[: 2 * NB] + (both[2 * NB :] + cross)


def solve_dimers(pairs, table, focks, coupling):
    matrix = (DIM_DEV, 2 * NB, 256)
    split = (DIM_DEV, 256, 256)
    return pl.pallas_call(
        solve_kernel,
        out_shape=(
            jax.ShapeDtypeStruct((N_TEAM * 32, 128), F32),
            jax.ShapeDtypeStruct((1, 128), F32),
        ),
        in_specs=[pl.BlockSpec(memory_space=SMEM)] + [pl.BlockSpec(memory_space=VMEM)] * 6,
        out_specs=(pl.BlockSpec(memory_space=VMEM), pl.BlockSpec(memory_space=VMEM)),
        scratch_shapes=[
            VMEM((2 * DIM_DEV, 128, 8), F32),
            VMEM((DIM_DEV, N_FRAG, 128), F32),
            VMEM((NB, NB), BF16),
            VMEM(matrix, F32),
            VMEM(matrix, F32),
            VMEM(split, BF16),
            VMEM(split, BF16),
            VMEM(split, BF16),
            VMEM(split, BF16),
        ],
        name="solve_dimers",
    )(pairs.reshape(2 * DIM_DEV), table, *focks, coupling)


def sort_kernel(arrived, own, next_1, next_2, energy):
    parts = [
        arrived[:, part * 8 : (part + 1) * 8, :].reshape(N_TEAM * 8, 128) for part in range(4)
    ]
    target = parts[2][:, ID_LANE : ID_LANE + 1].astype(jnp.int32)
    chosen = jnp.where(iota((128, 64), 1) == target, 1.0, 0.0).astype(BF16)
    value = jnp.concatenate(parts, axis=1)
    upper = value.astype(BF16)
    rest = value - upper.astype(F32)
    middle = rest.astype(BF16)
    lower = (rest - middle.astype(F32)).astype(BF16)
    total = jnp.zeros((64, 512), F32)
    for piece in (lower, middle, upper):
        total += lax.dot_general(
            chosen, piece, (((0,), (0,)), ((), ())), preferred_element_type=F32
        )
    own[...] = total[:16]
    next_1[...] = total[16:32].astype(BF16)
    next_2[...] = total[32:48].astype(BF16)
    summed = jnp.sum(parts[2], axis=0, keepdims=True)
    energy[...] = jnp.broadcast_to(summed, (8, 128))


def sort_blocks(arrived):
    return pl.pallas_call(
        sort_kernel,
        out_shape=(
            jax.ShapeDtypeStruct((16, 512), F32),
            jax.ShapeDtypeStruct((16, 512), BF16),
            jax.ShapeDtypeStruct((16, 512), BF16),
            jax.ShapeDtypeStruct((8, 128), F32),
        ),
        in_specs=[pl.BlockSpec(memory_space=VMEM)],
        out_specs=(pl.BlockSpec(memory_space=VMEM),) * 4,
        name="sort_blocks",
    )(arrived)


def join_kernel(own, from_1, from_2, energy, sent):
    total = own[...] + from_1[...].astype(F32) + from_2[...].astype(F32)
    lane = iota((8, 128), 1)
    mine = jnp.broadcast_to(energy[0:1, ENERGY_LANE : ENERGY_LANE + 1], (8, 128))
    for core in range(2):
        for part in range(4):
            rows = total[core * 8 : core * 8 + 8, part * 128 : (part + 1) * 128]
            if part == 2:
                rows = jnp.where(lane == SUM_LANE, mine, rows)
            for group in range(N_GRP):
                sent[2 * group + core, part * 8 : (part + 1) * 8, :] = rows


def join_blocks(own, from_1, from_2, energy):
    return pl.pallas_call(
        join_kernel,
        out_shape=jax.ShapeDtypeStruct((N_TEAM, 32, 128), F32),
        in_specs=[pl.BlockSpec(memory_space=VMEM)] * 4,
        out_specs=pl.BlockSpec(memory_space=VMEM),
        name="join_blocks",
    )(own, from_1, from_2, energy)


def unpack_kernel(arrived, dens, out, total, turned):
    for fragment in range(FRAG_DEV):
        upper = jnp.concatenate(
            [
                arrived[pl.ds(part * 8 + fragment, 16, stride=32), :]
                for part in range(4)
            ],
            axis=0,
        )
        turned[pl.ds(fragment, 32, stride=8), :] = jnp.concatenate(
            [upper.T[64:96, :], jnp.zeros((32, 64), F32)], axis=1
        )
    lane = iota((8, 128), 1)
    number = arrived[16:24, ONE_LANE : ONE_LANE + 1]
    number = jnp.broadcast_to(number, (8, 128))
    half_number = 0.5 * number

    def packed(row):
        start = (row % 16) * 32 + (row // 16) * 8
        return arrived[start : start + 8, :]

    def matrix_row(row):
        if row < 64:
            return packed(row)
        left = turned[(row - 64) * 8 : (row - 64) * 8 + 8, :]
        right = pltpu.roll(packed(row - 64), 96, 1)
        return jnp.where(lane < 64, left, right)

    def finish(tile, value):
        here = slice(tile * 128, (tile + 1) * 128)
        first = (-tile * 128) % (NB + 1)
        on_diagonal = jnp.logical_or(lane == first, lane == first + NB + 1)
        value = -0.5 * value - number * dens[:, here].astype(F32)
        out[:, here] = value + jnp.where(on_diagonal, half_number, 0.0)

    for quad in range(NB // 4):
        row_0 = matrix_row(4 * quad)
        row_1 = pltpu.roll(matrix_row(4 * quad + 1), 96, 1)
        row_2 = pltpu.roll(matrix_row(4 * quad + 2), 64, 1)
        row_3 = pltpu.roll(matrix_row(4 * quad + 3), 32, 1)
        finish(3 * quad, jnp.where(lane < 96, row_0, row_1))
        finish(3 * quad + 1, jnp.where(lane < 64, row_1, row_2))
        finish(3 * quad + 2, jnp.where(lane < 32, row_2, row_3))

    energy = jnp.zeros((1, 128), F32)
    for member in range(N_TEAM):
        energy += arrived[member * 32 + 16 : member * 32 + 17, :]
    total[...] = energy[:, SUM_LANE : SUM_LANE + 1]


def unpack_blocks(arrived, density):
    return pl.pallas_call(
        unpack_kernel,
        out_shape=(
            jax.ShapeDtypeStruct((FRAG_DEV, FLAT), F32),
            jax.ShapeDtypeStruct((1, 1), F32),
        ),
        in_specs=[pl.BlockSpec(memory_space=VMEM)] * 2,
        out_specs=(pl.BlockSpec(memory_space=VMEM),) * 2,
        scratch_shapes=[VMEM((256, 128), F32)],
        name="unpack_blocks",
    )(arrived.reshape(N_TEAM * 32, 128), density)


def energy_moves():
    moves = []
    for group in range(N_GRP):
        for pair in range(N_PAIR):
            for core in range(2):
                source = group * N_FRAG + pair * 2 + core
                away = (pair + 2 * group + core) % N_PAIR
                moves.append((source, group * N_FRAG + away * 2 + core))
    return moves


def per_device(density, fock_blocks, coupling, dimer_pairs, atom_counts, nuclear_charge, coords):
    table = atom_table(density, fock_blocks, nuclear_charge, atom_counts, coords)
    focks = [fock_blocks]
    for distance in range(1, REACH + 1):
        moves = [(index + distance, index) for index in range(N_FRAG - distance)]
        focks.append(lax.ppermute(fock_blocks, FRAG, moves))
    table = exchange(table, FRAG)
    focks = [fock.reshape(FRAG_DEV, NB, NB) for fock in focks]
    cross = coupling.reshape(DIM_DEV, NB, NB)
    sent, energies = solve_dimers(dimer_pairs, table, focks, cross)
    arrived = exchange(sent.reshape(N_TEAM, 32, 128), TEAM)
    own, next_1, next_2, energy = sort_blocks(arrived)
    from_1 = lax.ppermute(next_1, PAIR, [(index, index + 1) for index in range(N_PAIR - 1)])
    from_2 = lax.ppermute(next_2, PAIR, [(index, index + 2) for index in range(N_PAIR - 2)])
    energy = lax.ppermute(energy, GRP_FRAG, energy_moves())
    arrived = exchange(join_blocks(own, from_1, from_2, energy), TEAM)
    correction, total = unpack_blocks(arrived, density)
    return correction, energies[0, :DIM_DEV], total.reshape(())


def solution(mesh):
    finer = Mesh(
        mesh.devices.reshape(2, 4, 2, 8, 2), ("grp_0", "grp_1", "frag_0", "frag_1", "frag_2")
    )
    return jax.shard_map(
        per_device,
        mesh=finer,
        in_specs=(
            P(FRAG, None),
            P(FRAG, None),
            P(GRP_FRAG, None),
            P(GRP_FRAG, None),
            P(FRAG),
            P(FRAG),
            P(None, FRAG),
        ),
        out_specs=(P(FRAG, None), P(GRP_FRAG), P()),
        check_vma=False,
    )
```

time: 174 us -> 100 us (0.57)
  blocking collectives: 67.5 us -> 15.6 us
  Pallas kernels: 0 us -> 22.9 us
  matrix products: 22.6 us -> 0 us
  local copies, waits for them, and re-layouts: 19.7 us -> 8.06 us
  other arithmetic: 8.75 us -> 0 us
  starting transfers between devices: 43.3 us -> 36.5 us
  waiting for transfers between devices: 9.16 us -> 15.5 us
    psum x5 -> x0, blocking collectives: 44.9 us -> none  [by_axis(): value = lax.psum(value, axis)]
    pallas_call x0 -> x5, Pallas kernels: none -> 22.9 us  [the longest x1 15.5 us: solve_dimers(): pl.pallas_call(solve_kernel, out_shape=(jax.ShapeDtypeStruct((N_TEAM * 32...]
    dot_general x25 -> x0, matrix products: 22.6 us -> none  [the longest x12 11.2 us: purify(): jnp.dot(square, current, precision=FULL_PRECISION)]
    all_to_all x2, waiting for transfers between devices: 0.01 us -> 7.54 us  [exchange(): return lax.all_to_all(value, axis, split_axis=0, concat_axis=0, tiled=True)]
    all_to_all x1, blocking collectives: 22.6 us -> 15.6 us  [exchange(): return lax.all_to_all(value, axis, split_axis=0, concat_axis=0, tiled=True)]
    ppermute x9 -> x6, starting transfers between devices: 24.8 us -> 18.4 us  [the longest x1 5.59 us: per_device(): lax.ppermute(next_1, PAIR, [(index, index + 1) for index in range(N_PAIR...]
    gather x8 -> x0, local copies, waits for them, and re-layouts: 5.24 us -> none  [the longest x2 2.99 us: atom_table(): on_diagonal = jnp.diagonal(blocks, axis1=1, axis2=2)]
    reshape x5 -> x6, local copies, waits for them, and re-layouts: 1.01 us -> 4.85 us  [the longest x4 3.5 us: per_device(): focks = [fock.reshape(FRAG_DEV, NB, NB) for fock in focks]]
  transfers between devices with their start and end apart: 11 -> 8, of which waited for: 2 -> 4; matrix products, arithmetic and copies ran while one was open for 10% -> 5% of each run, Pallas kernels for 0% -> 0%
where the time goes in v1:
time: 100 us; the launch traced here: 99.3 us
  starting transfers between devices  36.5 us (36%)
  Pallas kernels  22.9 us (23%)
  blocking collectives  15.6 us (16%)
  waiting for transfers between devices  15.5 us (16%)
  local copies, waits for them, and re-layouts  8.06 us (8%)
    all_to_all x2, starting transfers between devices, exchange(): return lax.all_to_all(value, axis, split_axis=0, concat_axis=0, tiled=True)  18.1 us
    all_to_all x1, blocking collectives, exchange(): return lax.all_to_all(value, axis, split_axis=0, concat_axis=0, tiled=True)  15.6 us
    pallas_call x1, Pallas kernels, solve_dimers(): pl.pallas_call(solve_kernel, out_shape=(jax.ShapeDtypeStruct((N_TEAM * 32...  15.5 us
    all_to_all x2, waiting for transfers between devices, exchange(): return lax.all_to_all(value, axis, split_axis=0, concat_axis=0, tiled=True)  7.54 us
    ppermute x1, starting transfers between devices, per_device(): lax.ppermute(next_1, PAIR, [(index, index + 1) for index in range(N_PAIR...  5.59 us
    ppermute x3, starting transfers between devices, per_device(): focks.append(lax.ppermute(fock_blocks, FRAG, moves))  4.86 us
    ppermute x1, starting transfers between devices, per_device(): lax.ppermute(next_2, PAIR, [(index, index + 2) for index in range(N_PAIR...  4.83 us
    ppermute x3, waiting for transfers between devices, per_device(): focks.append(lax.ppermute(fock_blocks, FRAG, moves))  4.6 us
  transfers between devices with their start and end apart: 8, of which 4 were waited for; matrix products, arithmetic and copies ran while one was open for 5% of the time, Pallas kernels for 0%

profile of v1, /device:TPU:1, one launch (start us, length us, event | category | flops | bytes accessed | tf_op | source)
XLA Modules:
  0.0 99.3 jit_solution(11009577536765172674)
XLA Ops:
  0.6 1.9 %atom_table.1 = f32[32,8,128]{2,1,0:T(8,128)} custom-call(s32[8]{0:T(128)} %counts.1, bf16[8,9216]{1,0:T(8,128)(2,1)} %dens.3, bf16[8,9216]{1,0:T(8,128)(2,1)} %fock.1, f32[1,128]{1,0:T(1,128)} %bitcast.8, f32[3,128]{1,0:T(4,128)} %coords.1), custom_call_target="tpu_custom_call" | custom-call | tf_op jit(solution)/shard_map/atom_table/pallas_call | solution.py:90
  2.5 11.3 %all-to-all-start = ((f32[32,8,128]{2,1,0:T(8,128)}), f32[32,8,128]{2,1,0:T(8,128)S(1)}, u32[]{:S(2)}, u32[]{:S(2)}) async-start(f32[32,8,128]{2,1,0:T(8,128)} %atom_table.1), calls=%async_computation | async-start | bytes 262144 | tf_op jit(solution)/shard_map/all_to_all | solution.py:40
  13.8 2.3 %collective-permute-start = (bf16[8,9216]{1,0:T(8,128)(2,1)S(1)}, bf16[8,9216]{1,0:T(8,128)(2,1)S(1)}, u32[]{:S(2)}, u32[]{:S(2)}) collective-permute-start(bf16[8,9216]{1,0:T(8,128)(2,1)S(1)} %copy-done.1), channel_id=1, source_target_pairs={{1,0},{2,1},{3,2},{4,3},{5,4},{6,5},{7,6},{8,7},{9,8},{10,9},{11,1... | collective-permute-start | bytes 442376 | tf_op jit(solution)/shard_map/ppermute | solution.py:414
  16.1 1.3 %collective-permute-start.2 = (bf16[8,9216]{1,0:T(8,128)(2,1)S(1)}, bf16[8,9216]{1,0:T(8,128)(2,1)S(1)}, u32[]{:S(2)}, u32[]{:S(2)}) collective-permute-start(bf16[8,9216]{1,0:T(8,128)(2,1)S(1)} %copy-done.1), channel_id=1, source_target_pairs={{3,0},{4,1},{5,2},{6,3},{7,4},{8,5},{9,6},{10,7},{11,8},{12,9},{13... | collective-permute-start | bytes 442376 | tf_op jit(solution)/shard_map/ppermute | solution.py:414
  17.4 1.3 %collective-permute-start.1 = (bf16[8,9216]{1,0:T(8,128)(2,1)S(1)}, bf16[8,9216]{1,0:T(8,128)(2,1)S(1)}, u32[]{:S(2)}, u32[]{:S(2)}) collective-permute-start(bf16[8,9216]{1,0:T(8,128)(2,1)S(1)} %copy-done.1), channel_id=1, source_target_pairs={{2,0},{3,1},{4,2},{5,3},{6,4},{7,5},{8,6},{9,7},{10,8},{11,9},{12,... | collective-permute-start | bytes 442376 | tf_op jit(solution)/shard_map/ppermute | solution.py:414
  18.7 0.9 reshape.38.fock_0
  19.6 0.1 copy.11
  19.7 0.6 reshape.36.pairs
  20.3 0.8 reshape.42.coupling
  21.0 0.2 collective-permute-done
  21.2 0.9 reshape.39.fock_1
  22.1 4.4 %collective-permute-done.2 = bf16[8,9216]{1,0:T(8,128)(2,1)S(1)} collective-permute-done((bf16[8,9216]{1,0:T(8,128)(2,1)S(1)}, bf16[8,9216]{1,0:T(8,128)(2,1)S(1)}, u32[]{:S(2)}, u32[]{:S(2)}) %collective-permute-start.2) | collective-permute-done | bytes 147488 | tf_op jit(solution)/shard_map/ppermute | solution.py:414
  26.5 0.9 reshape.41.fock_3
  27.4 0.9 reshape.40.fock_2
  28.3 0.7 copy-done.2
  28.9 15.5 %solve_dimers.1 = (f32[512,128]{1,0:T(8,128)}, f32[1,128]{1,0:T(1,128)}) custom-call(s32[8]{0:T(128)} %reshape.36.pairs, f32[32,8,128]{2,1,0:T(8,128)} %copy-done.2, bf16[8,96,96]{2,1,0:T(8,128)(2,1)} %reshape.38.fock_0, bf16[8,96,96]{2,1,0:T(8,128)(2,1)} %reshape.39.fock_1, bf16[8,96,96]{2,1,0:T(8,128)(2,1)} %reshape.40.fock_2, ...), custom_call_target="tpu_custom_call" | custom-call | tf_op jit(solution)/shard_map/solve_dimers/pallas_call | solution.py:250
  44.4 15.6 %all_to_all.15.arrived = f32[16,32,128]{2,1,0:T(8,128)} all-to-all(f32[16,32,128]{2,1,0:T(8,128)} %bitcast.7), channel_id=1, replica_groups=mesh['grp_0'=2,'grp_1'=4,'frag_0'=2,'frag_1'=8,'frag_2'=2] {'grp_0','grp..., dimensions={0} | all-to-all | bytes 524288 | tf_op jit(solution)/shard_map/all_to_all | solution.py:40
  60.0 1.9 %sort_blocks.1 = (f32[16,512]{1,0:T(8,128)}, bf16[16,512]{1,0:T(8,128)(2,1)}, bf16[16,512]{1,0:T(8,128)(2,1)}, f32[8,128]{1,0:T(8,128)}) custom-call(f32[16,32,128]{2,1,0:T(8,128)} %all_to_all.15.arrived), custom_call_target="tpu_custom_call" | custom-call | tf_op jit(solution)/shard_map/sort_blocks/pallas_call | solution.py:297
  61.8 5.6 %collective-permute-start.3 = (bf16[16,512]{1,0:T(8,128)(2,1)}, bf16[16,512]{1,0:T(8,128)(2,1)S(1)}, u32[]{:S(2)}, u32[]{:S(2)}) collective-permute-start(bf16[16,512]{1,0:T(8,128)(2,1)} %get-tuple-element.13), channel_id=1, source_target_pairs={{0,2},{2,4},{4,6},{6,8},{8,10},{10,12},{12,14},{14,16},{16,18},{18... | collective-permute-start | bytes 49160 | tf_op jit(solution)/shard_map/ppermute | solution.py:421
  67.4 4.8 %collective-permute-start.4 = (bf16[16,512]{1,0:T(8,128)(2,1)}, bf16[16,512]{1,0:T(8,128)(2,1)S(1)}, u32[]{:S(2)}, u32[]{:S(2)}) collective-permute-start(bf16[16,512]{1,0:T(8,128)(2,1)} %get-tuple-element.14), channel_id=1, source_target_pairs={{0,4},{2,6},{4,8},{6,10},{8,12},{10,14},{12,16},{14,18},{16,20},{1... | collective-permute-start | bytes 49160 | tf_op jit(solution)/shard_map/ppermute | solution.py:422
  72.3 3.1 %collective-permute-start.5 = (f32[8,128]{1,0:T(8,128)S(1)}, f32[8,128]{1,0:T(8,128)S(1)}, u32[]{:S(2)}, u32[]{:S(2)}) collective-permute-start(f32[8,128]{1,0:T(8,128)S(1)} %copy-done.8), channel_id=1, source_target_pairs={{0,0},{1,3},{2,2},{3,5},{4,4},{5,7},{6,6},{7,9},{8,8},{9,11},{10,1... | collective-permute-start | bytes 12296 | tf_op jit(solution)/shard_map/ppermute | solution.py:423
  75.4 3.4 %collective-permute-done.5.energy = f32[8,128]{1,0:T(8,128)S(1)} collective-permute-done((f32[8,128]{1,0:T(8,128)S(1)}, f32[8,128]{1,0:T(8,128)S(1)}, u32[]{:S(2)}, u32[]{:S(2)}) %collective-permute-start.5) | collective-permute-done | bytes 4128 | tf_op jit(solution)/shard_map/ppermute | solution.py:423
  78.7 0.6 copy-done.6
  79.3 0.0 copy-done.4
  79.3 0.0 copy-done.5
  79.3 1.6 %join_blocks.1 = f32[16,32,128]{2,1,0:T(8,128)} custom-call(f32[16,512]{1,0:T(8,128)} %get-tuple-element.12.own, bf16[16,512]{1,0:T(8,128)(2,1)} %copy-done.4, bf16[16,512]{1,0:T(8,128)(2,1)} %copy-done.5, f32[8,128]{1,0:T(8,128)} %copy-done.6), custom_call_target="tpu_custom_call" | custom-call | tf_op jit(solution)/shard_map/join_blocks/pallas_call | solution.py:325
  80.9 6.9 %all-to-all-start.2 = ((f32[16,32,128]{2,1,0:T(8,128)}), f32[16,32,128]{2,1,0:T(8,128)S(1)}, u32[]{:S(2)}, u32[]{:S(2)}) async-start(f32[16,32,128]{2,1,0:T(8,128)} %join_blocks.1), calls=%async_computation.2 | async-start | bytes 524288 | tf_op jit(solution)/shard_map/all_to_all | solution.py:40
  87.8 0.6 copy-done.9
  88.5 0.5 slice_bitcast_fusion
  89.0 7.5 %all-to-all-done.2 = f32[16,32,128]{2,1,0:T(8,128)S(1)} async-done(((f32[16,32,128]{2,1,0:T(8,128)}), f32[16,32,128]{2,1,0:T(8,128)S(1)}, u32[]{:S(2)}, u32[]{:S(2)}) %all-to-all-start.2) | async-done | bytes 262176 | tf_op jit(solution)/shard_map/all_to_all | solution.py:40
  96.5 0.7 copy-done
  97.2 2.1 %unpack_blocks.1 = (f32[8,9216]{1,0:T(8,128)}, f32[1,1]{1,0:T(1,128)}) custom-call(f32[512,128]{1,0:T(8,128)} %bitcast.6, bf16[8,9216]{1,0:T(8,128)(2,1)} %dens.3), custom_call_target="tpu_custom_call" | custom-call | tf_op jit(solution)/shard_map/unpack_blocks/pallas_call | solution.py:385
  (18 shorter events, 0.0 us)
Async XLA Ops:
  2.5 11.3 %copy-start.1 = (bf16[8,9216]{1,0:T(8,128)(2,1)S(1)}, bf16[8,9216]{1,0:T(8,128)(2,1)}, u32[]{:S(2)}) copy-start(bf16[8,9216]{1,0:T(8,128)(2,1)} %fock.1) | copy-start | bytes 442372
  2.5 25.7 %all-to-all-start = ((f32[32,8,128]{2,1,0:T(8,128)}), f32[32,8,128]{2,1,0:T(8,128)S(1)}, u32[]{:S(2)}, u32[]{:S(2)}) async-start(f32[32,8,128]{2,1,0:T(8,128)} %atom_table.1), calls=%async_computation | async-start | bytes 262144 | tf_op jit(solution)/shard_map/all_to_all | solution.py:40
  13.8 5.8 %copy-start.7 = (s32[4,2]{0,1:T(2,128)S(1)}, s32[4,2]{0,1:T(2,128)}, u32[]{:S(2)}) copy-start(s32[4,2]{0,1:T(2,128)} %param.10) | copy-start | bytes 100
  13.8 6.5 %copy-start.3 = (bf16[4,9216]{1,0:T(4,128)(2,1)S(1)}, bf16[4,9216]{1,0:T(4,128)(2,1)}, u32[]{:S(2)}) copy-start(bf16[4,9216]{1,0:T(4,128)(2,1)} %param.9) | copy-start | bytes 221188
  13.8 7.4 %collective-permute-start = (bf16[8,9216]{1,0:T(8,128)(2,1)S(1)}, bf16[8,9216]{1,0:T(8,128)(2,1)S(1)}, u32[]{:S(2)}, u32[]{:S(2)}) collective-permute-start(bf16[8,9216]{1,0:T(8,128)(2,1)S(1)} %copy-done.1), channel_id=1, source_target_pairs={{1,0},{2,1},{3,2},{4,3},{5,4},{6,5},{7,6},{8,7},{9,8},{10,9},{11,1... | collective-permute-start | bytes 442376 | tf_op jit(solution)/shard_map/ppermute | solution.py:414
  16.1 10.4 %collective-permute-start.2 = (bf16[8,9216]{1,0:T(8,128)(2,1)S(1)}, bf16[8,9216]{1,0:T(8,128)(2,1)S(1)}, u32[]{:S(2)}, u32[]{:S(2)}) collective-permute-start(bf16[8,9216]{1,0:T(8,128)(2,1)S(1)} %copy-done.1), channel_id=1, source_target_pairs={{3,0},{4,1},{5,2},{6,3},{7,4},{8,5},{9,6},{10,7},{11,8},{12,9},{13... | collective-permute-start | bytes 442376 | tf_op jit(solution)/shard_map/ppermute | solution.py:414
  17.4 10.0 %collective-permute-start.1 = (bf16[8,9216]{1,0:T(8,128)(2,1)S(1)}, bf16[8,9216]{1,0:T(8,128)(2,1)S(1)}, u32[]{:S(2)}, u32[]{:S(2)}) collective-permute-start(bf16[8,9216]{1,0:T(8,128)(2,1)S(1)} %copy-done.1), channel_id=1, source_target_pairs={{2,0},{3,1},{4,2},{5,3},{6,4},{7,5},{8,6},{9,7},{10,8},{11,9},{12,... | collective-permute-start | bytes 442376 | tf_op jit(solution)/shard_map/ppermute | solution.py:414
  28.3 0.7 copy-start.2
  61.8 10.4 %copy-start.8 = (f32[8,128]{1,0:T(8,128)S(1)}, f32[8,128]{1,0:T(8,128)}, u32[]{:S(2)}) copy-start(f32[8,128]{1,0:T(8,128)} %get-tuple-element.15) | copy-start | bytes 12292
  61.8 16.9 %collective-permute-start.3 = (bf16[16,512]{1,0:T(8,128)(2,1)}, bf16[16,512]{1,0:T(8,128)(2,1)S(1)}, u32[]{:S(2)}, u32[]{:S(2)}) collective-permute-start(bf16[16,512]{1,0:T(8,128)(2,1)} %get-tuple-element.13), channel_id=1, source_target_pairs={{0,2},{2,4},{4,6},{6,8},{8,10},{10,12},{12,14},{14,16},{16,18},{18... | collective-permute-start | bytes 49160 | tf_op jit(solution)/shard_map/ppermute | solution.py:421
  67.4 11.3 %collective-permute-start.4 = (bf16[16,512]{1,0:T(8,128)(2,1)}, bf16[16,512]{1,0:T(8,128)(2,1)S(1)}, u32[]{:S(2)}, u32[]{:S(2)}) collective-permute-start(bf16[16,512]{1,0:T(8,128)(2,1)} %get-tuple-element.14), channel_id=1, source_target_pairs={{0,4},{2,6},{4,8},{6,10},{8,12},{10,14},{12,16},{14,18},{16,20},{1... | collective-permute-start | bytes 49160 | tf_op jit(solution)/shard_map/ppermute | solution.py:422
  72.3 6.5 %collective-permute-start.5 = (f32[8,128]{1,0:T(8,128)S(1)}, f32[8,128]{1,0:T(8,128)S(1)}, u32[]{:S(2)}, u32[]{:S(2)}) collective-permute-start(f32[8,128]{1,0:T(8,128)S(1)} %copy-done.8), channel_id=1, source_target_pairs={{0,0},{1,3},{2,2},{3,5},{4,4},{5,7},{6,6},{7,9},{8,8},{9,11},{10,1... | collective-permute-start | bytes 12296 | tf_op jit(solution)/shard_map/ppermute | solution.py:423
  78.7 0.6 copy-start.6
  78.7 0.6 copy-start.4
  78.7 0.6 copy-start.5
  80.9 15.6 %all-to-all-start.2 = ((f32[16,32,128]{2,1,0:T(8,128)}), f32[16,32,128]{2,1,0:T(8,128)S(1)}, u32[]{:S(2)}, u32[]{:S(2)}) async-start(f32[16,32,128]{2,1,0:T(8,128)} %join_blocks.1), calls=%async_computation.2 | async-start | bytes 524288 | tf_op jit(solution)/shard_map/all_to_all | solution.py:40
  87.8 0.7 copy-start.9
  96.5 0.7 copy-start

commit v2 on v1

--- a/solution.py
+++ b/solution.py
@@ -10,6 +10,7 @@
 NA = 16
 REACH = 3
 PURIF = 12
+UNROLL = 6
 FRAG_DEV = 8
 DIM_DEV = 4
 FLAT = NB * NB
@@ -96,37 +97,47 @@
     )(atom_counts, density, fock_blocks, nuclear_charge.reshape(1, 128), coords)
 
 
-def solve_kernel(
-    pairs, table, fock_0, fock_1, fock_2, fock_3, coupling, sent, energies,
-    columns, masked, fock_j, shifted, state, high, low, square_high, square_low,
-):
-    focks = (fock_0, fock_1, fock_2, fock_3)
-    base = (pairs[0] // FRAG_DEV) * FRAG_DEV
-    pair_base = (base // NA) * NA
+def unflatten(flat, matrices):
+    count = flat.shape[0]
+    lane = iota((count, 128), 1)
+    for quad in range(NB // 4):
+        tiles = []
+        for tile in range(3 * quad, 3 * quad + 3):
+            tiles.append(flat[:, tile * 128 : (tile + 1) * 128].astype(F32))
+        row_1 = jnp.where(lane < 96, tiles[1], tiles[0])
+        row_2 = jnp.where(lane < 64, tiles[2], tiles[1])
+        rows = [
+            tiles[0],
+            pltpu.roll(row_1, 32, 1),
+            pltpu.roll(row_2, 64, 1),
+            pltpu.roll(tiles[2], 96, 1),
+        ]
+        for offset, row in enumerate(rows):
+            start = (4 * quad + offset) * 8
+            matrices[start : start + count, :] = jnp.where(lane < NB, row, 0.0)
+
+
+def prepare_kernel(pairs, table, fock, coupling, fixed, starts, columns, masked, fock_rows, cross_rows):
+    unflatten(fock, fock_rows)
+    unflatten(coupling, cross_rows)
+    base = (pairs[0, 0] // FRAG_DEV) * FRAG_DEV
     lane = iota((NA, 128), 1)
     atom = iota((NA, 128), 0).astype(F32)
-
-    shifted[...] = jnp.zeros_like(shifted)
-    for buffer in (high, low, square_high, square_low):
-        for dimer in range(DIM_DEV):
-            buffer[dimer, NB:128, :] = jnp.zeros((128 - NB, 256), BF16)
-            buffer[dimer, 128 + NB :, :] = jnp.zeros((128 - NB, 256), BF16)
 
     source = iota((N_FRAG, 128), 0) * FRAG_DEV + iota((N_FRAG, 128), 1) // NA
     charges = table[:, 0, :]
     for dimer in range(DIM_DEV):
-        first, second = pairs[2 * dimer], pairs[2 * dimer + 1]
-        hidden = jnp.logical_or(source == first, source == second)
+        hidden = jnp.logical_or(source == pairs[dimer, 0], source == pairs[dimer, 1])
         masked[dimer] = jnp.where(hidden, 0.0, charges)
         for side in range(2):
-            fragment = pairs[2 * dimer + side]
+            fragment = pairs[dimer, side]
             columns[2 * dimer + side] = table[fragment // FRAG_DEV].T
 
-    shifts, starts = [], []
+    small_eye = iota((NB, 128), 0) == iota((NB, 128), 1)
     for dimer in range(DIM_DEV):
         own, places = [], []
         for side in range(2):
-            local = pl.multiple_of((pairs[2 * dimer + side] % FRAG_DEV) * NA, NA)
+            local = pl.multiple_of((pairs[dimer, side] % FRAG_DEV) * NA, NA)
             mine = columns[2 * dimer + side, pl.ds(local, NA), :]
             own.append(mine)
             places.append([jnp.broadcast_to(mine[:, k : k + 1], (NA, 128)) for k in (1, 2, 3)])
@@ -152,32 +163,63 @@
             scaled = lane.astype(F32) * count
             inside = jnp.logical_and(atom * NB <= scaled, scaled < (atom + 1.0) * NB)
             inside = jnp.logical_and(inside, lane < NB)
-            shifts.append(jnp.sum(jnp.where(inside, potential, 0.0), axis=0, keepdims=True))
+            shift = jnp.sum(jnp.where(inside, potential, 0.0), axis=0, keepdims=True)
+            shift = jnp.where(small_eye, shift, 0.0)
+            if side == 0:
+                held = pairs[dimer, 0] - base
+                shift += fock_rows[pl.ds(held, NB, stride=8), :]
+            fixed[dimer, side * NB : (side + 1) * NB, side * 128 : (side + 1) * 128] = shift
             start += jnp.sum(potential * population + trace, axis=0, keepdims=True)
-        starts.append(start)
-
-    small_eye = iota((NB, NB), 0) == iota((NB, NB), 1)
+        starts[dimer : dimer + 1, :] = jnp.broadcast_to(start, (1, 128))
+        cross = cross_rows[pl.ds(dimer, NB, stride=8), :]
+        fixed[dimer, :NB, 128:256] = cross
+        fixed[dimer, NB:, :128] = jnp.concatenate(
+            [cross.T[:NB, :], jnp.zeros((NB, 128 - NB), F32)], axis=1
+        )
+
+
+def prepare_dimers(pairs, table, fock, coupling):
+    return pl.pallas_call(
+        prepare_kernel,
+        out_shape=(
+            jax.ShapeDtypeStruct((DIM_DEV, 2 * NB, 256), F32),
+            jax.ShapeDtypeStruct((8, 128), F32),
+        ),
+        in_specs=[pl.BlockSpec(memory_space=SMEM)] + [pl.BlockSpec(memory_space=VMEM)] * 3,
+        out_specs=(pl.BlockSpec(memory_space=VMEM),) * 2,
+        scratch_shapes=[
+            VMEM((2 * DIM_DEV, 128, 8), F32),
+            VMEM((DIM_DEV, N_FRAG, 128), F32),
+            VMEM((8 * NB, 128), F32),
+            VMEM((8 * NB, 128), F32),
+        ],
+        compiler_params=pltpu.CompilerParams(vmem_limit_bytes=8 << 20),
+        name="prepare_dimers",
+    )(pairs, table, fock, coupling)
+
+
+def solve_kernel(
+    pairs, fixed, starts, fock_0, fock_1, fock_2, fock_3, sent, energies,
+    fock_rows, shifted, state, high, low, square_high, square_low,
+):
+    for far, fock in enumerate((fock_0, fock_1, fock_2, fock_3)):
+        unflatten(fock, fock_rows.at[far])
+    base = (pairs[0, 0] // FRAG_DEV) * FRAG_DEV
+    pair_base = (base // NA) * NA
+    for buffer in (high, low, square_high, square_low):
+        for dimer in range(DIM_DEV):
+            buffer[dimer, NB:128, :] = jnp.zeros((128 - NB, 256), BF16)
+            buffer[dimer, 128 + NB :, :] = jnp.zeros((128 - NB, 256), BF16)
+
     rows, cols = iota((2 * NB, 256), 0), iota((2 * NB, 256), 1)
     eye = cols == jnp.where(rows < NB, rows, rows + (128 - NB))
-    centres, widths = [], []
+    centres = []
     for dimer in range(DIM_DEV):
-        second = pairs[2 * dimer + 1] - base
-        for far in range(REACH + 1):
-
-            @pl.when(second // FRAG_DEV == far)
-            def _(far=far, second=second):
-                fock_j[...] = focks[far][second % FRAG_DEV]
-
-        cross = coupling[dimer].astype(F32)
-        for side in range(2):
-            at, to = side * NB, side * 128
-            part = fock_0[pairs[2 * dimer] - base] if side == 0 else fock_j[...]
-            shift = shifts[2 * dimer + side][:, :NB]
-            shifted[dimer, at : at + NB, to : to + NB] = part.astype(F32) + jnp.where(
-                small_eye, shift, 0.0
-            )
-        shifted[dimer, :NB, 128 : 128 + NB] = cross
-        shifted[dimer, NB:, :NB] = cross.T
+        held = pairs[dimer, 1] - base
+        part = fock_rows[held // FRAG_DEV, pl.ds(held % FRAG_DEV, NB, stride=8), :]
+        shifted[dimer, :NB, :] = fixed[dimer, :NB, :]
+        shifted[dimer, NB:, :128] = fixed[dimer, NB:, :128]
+        shifted[dimer, NB:, 128:] = fixed[dimer, NB:, 128:] + part
         fock = shifted[dimer]
         trace = jnp.sum(jnp.where(eye, fock, 0.0), axis=(0, 1), keepdims=True)
         centre = trace / (2.0 * NB)
@@ -200,23 +242,21 @@
             keep(high, low, dimer, later)
         return carry
 
-    lax.fori_loop(0, PURIF, purify, 0)
-
-    last = jnp.zeros((1, 128), F32)
-    row_lane = iota((1, 128), 1)
+    lax.fori_loop(0, PURIF, purify, 0, unroll=UNROLL)
+
     lane_16 = iota((16, 128), 1)
     for dimer in range(DIM_DEV):
         final = state[dimer]
         overlap = jnp.sum(final * shifted[dimer], axis=(0, 1), keepdims=True)
         trace = jnp.sum(jnp.where(eye, final, 0.0), axis=(0, 1), keepdims=True)
         centre = centres[dimer]
-        energy = 0.5 * (2.0 * NB * centre - overlap - centre * trace) - starts[dimer]
-        last = jnp.where(row_lane == dimer, energy, last)
+        energy = 0.5 * (2.0 * NB * centre - overlap - centre * trace) - starts[dimer : dimer + 1, 0:1]
+        energies[dimer] = jnp.sum(energy)
         for side in range(2):
             slot = side * DIM_DEV + dimer
             block = final[side * NB : (side + 1) * NB, side * 128 : (side + 1) * 128]
             corner = pltpu.roll(block[64:96, :], 32, 1)
-            target = (pairs[2 * dimer + side] - pair_base).astype(F32)
+            target = (pairs[dimer, side] - pair_base).astype(F32)
             beside = jnp.where(lane_16 == ID_LANE, target, 0.0)
             beside = jnp.where(lane_16 == ONE_LANE, 1.0, beside)
             if side == 0:
@@ -226,7 +266,6 @@
                 other = corner[16 * part : 16 * (part + 1), :] if part < 2 else beside
                 piece = jnp.where(lane_16 < NB, piece, other)
                 sent[pl.ds(part * 8 + slot, 16, stride=32), :] = piece
-    energies[...] = last
 
 
 def keep(high, low, dimer, value):
@@ -244,21 +283,19 @@
     return both[: 2 * NB] + (both[2 * NB :] + cross)
 
 
-def solve_dimers(pairs, table, focks, coupling):
+def solve_dimers(pairs, fixed, starts, focks):
     matrix = (DIM_DEV, 2 * NB, 256)
     split = (DIM_DEV, 256, 256)
     return pl.pallas_call(
         solve_kernel,
         out_shape=(
             jax.ShapeDtypeStruct((N_TEAM * 32, 128), F32),
-            jax.ShapeDtypeStruct((1, 128), F32),
+            jax.ShapeDtypeStruct((DIM_DEV,), F32),
         ),
         in_specs=[pl.BlockSpec(memory_space=SMEM)] + [pl.BlockSpec(memory_space=VMEM)] * 6,
-        out_specs=(pl.BlockSpec(memory_space=VMEM), pl.BlockSpec(memory_space=VMEM)),
+        out_specs=(pl.BlockSpec(memory_space=VMEM), pl.BlockSpec(memory_space=SMEM)),
         scratch_shapes=[
-            VMEM((2 * DIM_DEV, 128, 8), F32),
-            VMEM((DIM_DEV, N_FRAG, 128), F32),
-            VMEM((NB, NB), BF16),
+            VMEM((REACH + 1, 8 * NB, 128), F32),
             VMEM(matrix, F32),
             VMEM(matrix, F32),
             VMEM(split, BF16),
@@ -266,8 +303,9 @@
             VMEM(split, BF16),
             VMEM(split, BF16),
         ],
+        compiler_params=pltpu.CompilerParams(vmem_limit_bytes=20 << 20),
         name="solve_dimers",
-    )(pairs.reshape(2 * DIM_DEV), table, *focks, coupling)
+    )(pairs, fixed, starts, *focks)
 
 
 def sort_kernel(arrived, own, next_1, next_2, energy):
@@ -304,6 +342,7 @@
         ),
         in_specs=[pl.BlockSpec(memory_space=VMEM)],
         out_specs=(pl.BlockSpec(memory_space=VMEM),) * 4,
+        compiler_params=pltpu.CompilerParams(vmem_limit_bytes=4 << 20),
         name="sort_blocks",
     )(arrived)
 
@@ -327,6 +366,7 @@
         out_shape=jax.ShapeDtypeStruct((N_TEAM, 32, 128), F32),
         in_specs=[pl.BlockSpec(memory_space=VMEM)] * 4,
         out_specs=pl.BlockSpec(memory_space=VMEM),
+        compiler_params=pltpu.CompilerParams(vmem_limit_bytes=4 << 20),
         name="join_blocks",
     )(own, from_1, from_2, energy)
 
@@ -391,6 +431,7 @@
         in_specs=[pl.BlockSpec(memory_space=VMEM)] * 2,
         out_specs=(pl.BlockSpec(memory_space=VMEM),) * 2,
         scratch_shapes=[VMEM((256, 128), F32)],
+        compiler_params=pltpu.CompilerParams(vmem_limit_bytes=4 << 20),
         name="unpack_blocks",
     )(arrived.reshape(N_TEAM * 32, 128), density)
 
@@ -413,9 +454,8 @@
         moves = [(index + distance, index) for index in range(N_FRAG - distance)]
         focks.append(lax.ppermute(fock_blocks, FRAG, moves))
     table = exchange(table, FRAG)
-    focks = [fock.reshape(FRAG_DEV, NB, NB) for fock in focks]
-    cross = coupling.reshape(DIM_DEV, NB, NB)
-    sent, energies = solve_dimers(dimer_pairs, table, focks, cross)
+    fixed, starts = prepare_dimers(dimer_pairs, table, fock_blocks, coupling)
+    sent, energies = solve_dimers(dimer_pairs, fixed, starts, focks)
     arrived = exchange(sent.reshape(N_TEAM, 32, 128), TEAM)
     own, next_1, next_2, energy = sort_blocks(arrived)
     from_1 = lax.ppermute(next_1, PAIR, [(index, index + 1) for index in range(N_PAIR - 1)])
@@ -423,7 +463,7 @@
     energy = lax.ppermute(energy, GRP_FRAG, energy_moves())
     arrived = exchange(join_blocks(own, from_1, from_2, energy), TEAM)
     correction, total = unpack_blocks(arrived, density)
-    return correction, energies[0, :DIM_DEV], total.reshape(())
+    return correction, energies, total.reshape(())
 
 
 def solution(mesh):

time: 100 us -> 85.6 us (0.86)
  blocking collectives: 15.6 us -> 30.5 us
  starting transfers between devices: 36.5 us -> 27 us
  local copies, waits for them, and re-layouts: 8.06 us -> 0.11 us
  Pallas kernels: 22.9 us -> 16.3 us
  waiting for transfers between devices: 15.5 us -> 10.6 us
    all_to_all x1 -> x2, blocking collectives: 15.6 us -> 30.5 us  [exchange(): return lax.all_to_all(value, axis, split_axis=0, concat_axis=0, tiled=True)]
    all_to_all x2 -> x1, starting transfers between devices: 18.1 us -> 11.3 us  [exchange(): return lax.all_to_all(value, axis, split_axis=0, concat_axis=0, tiled=True)]
    pallas_call x1, Pallas kernels: 15.5 us -> 10.2 us  [solve_dimers(): pl.pallas_call(solve_kernel, out_shape=(jax.ShapeDtypeStruct((N_TEAM * 32...]
    reshape x6 -> x0, local copies, waits for them, and re-layouts: 4.85 us -> none  [the longest x4 3.5 us: per_device(): focks = [fock.reshape(FRAG_DEV, NB, NB) for fock in focks]]
    all_to_all x2 -> x1, waiting for transfers between devices: 7.54 us -> 4.13 us  [exchange(): return lax.all_to_all(value, axis, split_axis=0, concat_axis=0, tiled=True)]
    pallas_call x0 -> x1, Pallas kernels: none -> 2.7 us  [prepare_dimers(): pl.pallas_call(prepare_kernel, out_shape=(jax.ShapeDtypeStruct((DIM_DEV,...]
    unnamed x21 -> x9, local copies, waits for them, and re-layouts: 2.71 us -> 0.11 us
    ppermute x1, starting transfers between devices: 5.59 us -> 3 us  [per_device(): lax.ppermute(next_1, PAIR, [(index, index + 1) for index in range(N_PAIR...]
  transfers between devices with their start and end apart: 8 -> 7, of which waited for: 4 -> 3; matrix products, arithmetic and copies ran while one was open for 5% -> 0% of each run, Pallas kernels for 0% -> 3%
where the time goes in v2:
time: 85.6 us; the launch traced here: 85.2 us
  blocking collectives  30.5 us (36%)
  starting transfers between devices  27 us (32%)
  Pallas kernels  16.3 us (19%)
  waiting for transfers between devices  10.6 us (12%)
    all_to_all x2, blocking collectives, exchange(): return lax.all_to_all(value, axis, split_axis=0, concat_axis=0, tiled=True)  30.5 us
    all_to_all x1, starting transfers between devices, exchange(): return lax.all_to_all(value, axis, split_axis=0, concat_axis=0, tiled=True)  11.3 us
    pallas_call x1, Pallas kernels, solve_dimers(): pl.pallas_call(solve_kernel, out_shape=(jax.ShapeDtypeStruct((N_TEAM * 32...  10.2 us
    ppermute x3, starting transfers between devices, per_device(): focks.append(lax.ppermute(fock_blocks, FRAG, moves))  4.73 us
    ppermute x1, starting transfers between devices, per_device(): lax.ppermute(next_2, PAIR, [(index, index + 2) for index in range(N_PAIR...  4.53 us
    all_to_all x1, waiting for transfers between devices, exchange(): return lax.all_to_all(value, axis, split_axis=0, concat_axis=0, tiled=True)  4.13 us
    ppermute x1, starting transfers between devices, per_device(): energy = lax.ppermute(energy, GRP_FRAG, energy_moves())  3.49 us
    ppermute x3, waiting for transfers between devices, per_device(): focks.append(lax.ppermute(fock_blocks, FRAG, moves))  3.48 us
  transfers between devices with their start and end apart: 7, of which 3 were waited for; matrix products, arithmetic and copies ran while one was open for 0% of the time, Pallas kernels for 3%

profile of v2, /device:TPU:1, one launch (start us, length us, event | category | flops | bytes accessed | tf_op | source)
XLA Modules:
  0.0 85.2 jit_solution(16740862158714417577)
XLA Ops:
  0.6 1.9 %atom_table.1 = f32[32,8,128]{2,1,0:T(8,128)} custom-call(s32[8]{0:T(128)} %counts.1, bf16[8,9216]{1,0:T(8,128)(2,1)} %dens.3, bf16[8,9216]{1,0:T(8,128)(2,1)} %fock_0.1, f32[1,128]{1,0:T(1,128)} %bitcast.6, f32[3,128]{1,0:T(4,128)} %coords.1), custom_call_target="tpu_custom_call" | custom-call | tf_op jit(solution)/shard_map/atom_table/pallas_call | solution.py:91
  2.5 0.0 copy-start
  2.5 0.0 copy-start.3
  2.5 0.0 copy-start.2
  2.5 11.3 %all-to-all-start = ((f32[32,8,128]{2,1,0:T(8,128)}), f32[32,8,128]{2,1,0:T(8,128)S(1)}, u32[]{:S(2)}, u32[]{:S(2)}) async-start(f32[32,8,128]{2,1,0:T(8,128)} %atom_table.1), calls=%async_computation | async-start | bytes 262144 | tf_op jit(solution)/shard_map/all_to_all | solution.py:41
  13.8 0.0 copy-done
  13.8 1.3 %collective-permute-start.1 = (bf16[8,9216]{1,0:T(8,128)(2,1)S(1)}, bf16[8,9216]{1,0:T(8,128)(2,1)S(1)}, u32[]{:S(2)}, u32[]{:S(2)}) collective-permute-start(bf16[8,9216]{1,0:T(8,128)(2,1)S(1)} %copy-done), channel_id=1, source_target_pairs={{2,0},{3,1},{4,2},{5,3},{6,4},{7,5},{8,6},{9,7},{10,8},{11,9},{12,... | collective-permute-start | bytes 442376 | tf_op jit(solution)/shard_map/ppermute | solution.py:455
  15.1 2.1 %collective-permute-start = (bf16[8,9216]{1,0:T(8,128)(2,1)S(1)}, bf16[8,9216]{1,0:T(8,128)(2,1)S(1)}, u32[]{:S(2)}, u32[]{:S(2)}) collective-permute-start(bf16[8,9216]{1,0:T(8,128)(2,1)S(1)} %copy-done), channel_id=1, source_target_pairs={{1,0},{2,1},{3,2},{4,3},{5,4},{6,5},{7,6},{8,7},{9,8},{10,9},{11,1... | collective-permute-start | bytes 442376 | tf_op jit(solution)/shard_map/ppermute | solution.py:455
  17.3 1.3 %collective-permute-start.2 = (bf16[8,9216]{1,0:T(8,128)(2,1)S(1)}, bf16[8,9216]{1,0:T(8,128)(2,1)S(1)}, u32[]{:S(2)}, u32[]{:S(2)}) collective-permute-start(bf16[8,9216]{1,0:T(8,128)(2,1)S(1)} %copy-done), channel_id=1, source_target_pairs={{3,0},{4,1},{5,2},{6,3},{7,4},{8,5},{9,6},{10,7},{11,8},{12,9},{13... | collective-permute-start | bytes 442376 | tf_op jit(solution)/shard_map/ppermute | solution.py:455
  18.6 0.0 copy-done.3
  18.6 0.1 copy.11.pairs
  18.7 4.1 %all-to-all-done.table = f32[32,8,128]{2,1,0:T(8,128)S(1)} async-done(((f32[32,8,128]{2,1,0:T(8,128)}), f32[32,8,128]{2,1,0:T(8,128)S(1)}, u32[]{:S(2)}, u32[]{:S(2)}) %all-to-all-start) | async-done | bytes 131104 | tf_op jit(solution)/shard_map/all_to_all | solution.py:41
  22.8 0.0 copy-done.2
  22.8 2.7 %prepare_dimers.1 = (f32[4,192,256]{2,1,0:T(8,128)S(1)}, f32[8,128]{1,0:T(8,128)S(1)}) custom-call(s32[4,2]{1,0:T(4,128)S(1)} %copy.11.pairs, f32[32,8,128]{2,1,0:T(8,128)S(1)} %all-to-all-done.table, bf16[8,9216]{1,0:T(8,128)(2,1)S(1)} %copy-done, bf16[4,9216]{1,0:T(4,128)(2,1)S(1)} %copy-done.2), custom_call_target="tpu_custom_call" | custom-call | tf_op jit(solution)/shard_map/prepare_dimers/pallas_call | solution.py:182
  25.5 0.0 collective-permute-done.1.fock_2
  25.5 0.0 collective-permute-done.fock_1
  25.5 3.5 %collective-permute-done.2.fock_3 = bf16[8,9216]{1,0:T(8,128)(2,1)S(1)} collective-permute-done((bf16[8,9216]{1,0:T(8,128)(2,1)S(1)}, bf16[8,9216]{1,0:T(8,128)(2,1)S(1)}, u32[]{:S(2)}, u32[]{:S(2)}) %collective-permute-start.2) | collective-permute-done | bytes 147488 | tf_op jit(solution)/shard_map/ppermute | solution.py:455
  29.0 10.2 %solve_dimers.1 = (f32[512,128]{1,0:T(8,128)S(1)}, f32[4]{0:T(128)}) custom-call(s32[4,2]{1,0:T(4,128)S(1)} %copy.11.pairs, f32[4,192,256]{2,1,0:T(8,128)S(1)} %get-tuple-element.13.fixed, f32[8,128]{1,0:T(8,128)S(1)} %get-tuple-element.14.starts, bf16[8,9216]{1,0:T(8,128)(2,1)S(1)} %copy-done, bf16[8,9216]{1,0:T(8,128)(2,1)S(1)} %collective-permute-done.fock_1, ...), custom_call_target="tpu_custom_call" | custom-call | tf_op jit(solution)/shard_map/solve_dimers/pallas_call | solution.py:289
  39.2 15.3 %all_to_all.15.arrived = f32[16,32,128]{2,1,0:T(8,128)S(1)} all-to-all(f32[16,32,128]{2,1,0:T(8,128)S(1)} %bitcast.5), channel_id=1, replica_groups=mesh['grp_0'=2,'grp_1'=4,'frag_0'=2,'frag_1'=8,'frag_2'=2] {'grp_0','grp..., dimensions={0} | all-to-all | bytes 524288 | tf_op jit(solution)/shard_map/all_to_all | solution.py:41
  54.4 0.3 sort_blocks.1
  54.7 3.0 %collective-permute-start.3 = (bf16[16,512]{1,0:T(8,128)(2,1)S(1)}, bf16[16,512]{1,0:T(8,128)(2,1)S(1)}, u32[]{:S(2)}, u32[]{:S(2)}) collective-permute-start(bf16[16,512]{1,0:T(8,128)(2,1)S(1)} %get-tuple-element.17), channel_id=1, source_target_pairs={{0,2},{2,4},{4,6},{6,8},{8,10},{10,12},{12,14},{14,16},{16,18},{18... | collective-permute-start | bytes 49160 | tf_op jit(solution)/shard_map/ppermute | solution.py:461
  57.8 4.5 %collective-permute-start.4 = (bf16[16,512]{1,0:T(8,128)(2,1)S(1)}, bf16[16,512]{1,0:T(8,128)(2,1)S(1)}, u32[]{:S(2)}, u32[]{:S(2)}) collective-permute-start(bf16[16,512]{1,0:T(8,128)(2,1)S(1)} %get-tuple-element.18), channel_id=1, source_target_pairs={{0,4},{2,6},{4,8},{6,10},{8,12},{10,14},{12,16},{14,18},{16,20},{1... | collective-permute-start | bytes 49160 | tf_op jit(solution)/shard_map/ppermute | solution.py:462
  62.3 3.5 %collective-permute-start.5 = (f32[8,128]{1,0:T(8,128)S(1)}, f32[8,128]{1,0:T(8,128)S(1)}, u32[]{:S(2)}, u32[]{:S(2)}) collective-permute-start(f32[8,128]{1,0:T(8,128)S(1)} %get-tuple-element.19), channel_id=1, source_target_pairs={{0,0},{1,3},{2,2},{3,5},{4,4},{5,7},{6,6},{7,9},{8,8},{9,11},{10,1... | collective-permute-start | bytes 12296 | tf_op jit(solution)/shard_map/ppermute | solution.py:463
  65.8 3.0 %collective-permute-done.5.energy = f32[8,128]{1,0:T(8,128)S(1)} collective-permute-done((f32[8,128]{1,0:T(8,128)S(1)}, f32[8,128]{1,0:T(8,128)S(1)}, u32[]{:S(2)}, u32[]{:S(2)}) %collective-permute-start.5) | collective-permute-done | bytes 4128 | tf_op jit(solution)/shard_map/ppermute | solution.py:463
  68.8 0.0 collective-permute-done.3.from_1
  68.8 0.0 collective-permute-done.4.from_2
  68.8 0.1 join_blocks.1
  68.9 0.0 copy-start.1
  68.9 15.2 %all_to_all.16 = f32[16,32,128]{2,1,0:T(8,128)S(1)} all-to-all(f32[16,32,128]{2,1,0:T(8,128)S(1)} %join_blocks.1), channel_id=1, replica_groups=mesh['grp_0'=2,'grp_1'=4,'frag_0'=2,'frag_1'=8,'frag_2'=2] {'grp_0','grp..., dimensions={0} | all-to-all | bytes 524288 | tf_op jit(solution)/shard_map/all_to_all | solution.py:41
  84.1 0.0 copy-done.1
  84.1 1.1 %unpack_blocks.1 = (f32[8,9216]{1,0:T(8,128)}, f32[1,1]{1,0:T(1,128)}) custom-call(f32[512,128]{1,0:T(8,128)S(1)} %bitcast.4, bf16[8,9216]{1,0:T(8,128)(2,1)S(1)} %copy-done.1), custom_call_target="tpu_custom_call" | custom-call | tf_op jit(solution)/shard_map/unpack_blocks/pallas_call | solution.py:425
Async XLA Ops:
  2.5 11.3 %copy-start = (bf16[8,9216]{1,0:T(8,128)(2,1)S(1)}, bf16[8,9216]{1,0:T(8,128)(2,1)}, u32[]{:S(2)}) copy-start(bf16[8,9216]{1,0:T(8,128)(2,1)} %fock_0.1) | copy-start | bytes 442372
  2.5 16.0 %copy-start.3 = (s32[4,2]{0,1:T(2,128)S(1)}, s32[4,2]{0,1:T(2,128)}, u32[]{:S(2)}) copy-start(s32[4,2]{0,1:T(2,128)} %param.10) | copy-start | bytes 100
  2.5 20.3 %copy-start.2 = (bf16[4,9216]{1,0:T(4,128)(2,1)S(1)}, bf16[4,9216]{1,0:T(4,128)(2,1)}, u32[]{:S(2)}) copy-start(bf16[4,9216]{1,0:T(4,128)(2,1)} %coupling.1) | copy-start | bytes 221188
  2.5 20.3 %all-to-all-start = ((f32[32,8,128]{2,1,0:T(8,128)}), f32[32,8,128]{2,1,0:T(8,128)S(1)}, u32[]{:S(2)}, u32[]{:S(2)}) async-start(f32[32,8,128]{2,1,0:T(8,128)} %atom_table.1), calls=%async_computation | async-start | bytes 262144 | tf_op jit(solution)/shard_map/all_to_all | solution.py:41
  13.8 11.7 %collective-permute-start.1 = (bf16[8,9216]{1,0:T(8,128)(2,1)S(1)}, bf16[8,9216]{1,0:T(8,128)(2,1)S(1)}, u32[]{:S(2)}, u32[]{:S(2)}) collective-permute-start(bf16[8,9216]{1,0:T(8,128)(2,1)S(1)} %copy-done), channel_id=1, source_target_pairs={{2,0},{3,1},{4,2},{5,3},{6,4},{7,5},{8,6},{9,7},{10,8},{11,9},{12,... | collective-permute-start | bytes 442376 | tf_op jit(solution)/shard_map/ppermute | solution.py:455
  15.1 10.4 %collective-permute-start = (bf16[8,9216]{1,0:T(8,128)(2,1)S(1)}, bf16[8,9216]{1,0:T(8,128)(2,1)S(1)}, u32[]{:S(2)}, u32[]{:S(2)}) collective-permute-start(bf16[8,9216]{1,0:T(8,128)(2,1)S(1)} %copy-done), channel_id=1, source_target_pairs={{1,0},{2,1},{3,2},{4,3},{5,4},{6,5},{7,6},{8,7},{9,8},{10,9},{11,1... | collective-permute-start | bytes 442376 | tf_op jit(solution)/shard_map/ppermute | solution.py:455
  17.3 11.7 %collective-permute-start.2 = (bf16[8,9216]{1,0:T(8,128)(2,1)S(1)}, bf16[8,9216]{1,0:T(8,128)(2,1)S(1)}, u32[]{:S(2)}, u32[]{:S(2)}) collective-permute-start(bf16[8,9216]{1,0:T(8,128)(2,1)S(1)} %copy-done), channel_id=1, source_target_pairs={{3,0},{4,1},{5,2},{6,3},{7,4},{8,5},{9,6},{10,7},{11,8},{12,9},{13... | collective-permute-start | bytes 442376 | tf_op jit(solution)/shard_map/ppermute | solution.py:455
  54.7 14.0 %collective-permute-start.3 = (bf16[16,512]{1,0:T(8,128)(2,1)S(1)}, bf16[16,512]{1,0:T(8,128)(2,1)S(1)}, u32[]{:S(2)}, u32[]{:S(2)}) collective-permute-start(bf16[16,512]{1,0:T(8,128)(2,1)S(1)} %get-tuple-element.17), channel_id=1, source_target_pairs={{0,2},{2,4},{4,6},{6,8},{8,10},{10,12},{12,14},{14,16},{16,18},{18... | collective-permute-start | bytes 49160 | tf_op jit(solution)/shard_map/ppermute | solution.py:461
  57.8 11.0 %collective-permute-start.4 = (bf16[16,512]{1,0:T(8,128)(2,1)S(1)}, bf16[16,512]{1,0:T(8,128)(2,1)S(1)}, u32[]{:S(2)}, u32[]{:S(2)}) collective-permute-start(bf16[16,512]{1,0:T(8,128)(2,1)S(1)} %get-tuple-element.18), channel_id=1, source_target_pairs={{0,4},{2,6},{4,8},{6,10},{8,12},{10,14},{12,16},{14,18},{16,20},{1... | collective-permute-start | bytes 49160 | tf_op jit(solution)/shard_map/ppermute | solution.py:462
  62.3 6.5 %collective-permute-start.5 = (f32[8,128]{1,0:T(8,128)S(1)}, f32[8,128]{1,0:T(8,128)S(1)}, u32[]{:S(2)}, u32[]{:S(2)}) collective-permute-start(f32[8,128]{1,0:T(8,128)S(1)} %get-tuple-element.19), channel_id=1, source_target_pairs={{0,0},{1,3},{2,2},{3,5},{4,4},{5,7},{6,6},{7,9},{8,8},{9,11},{10,1... | collective-permute-start | bytes 12296 | tf_op jit(solution)/shard_map/ppermute | solution.py:463
  68.9 15.2 %copy-start.1 = (bf16[8,9216]{1,0:T(8,128)(2,1)S(1)}, bf16[8,9216]{1,0:T(8,128)(2,1)}, u32[]{:S(2)}) copy-start(bf16[8,9216]{1,0:T(8,128)(2,1)} %dens.3) | copy-start | bytes 442372

commit v3 on v2

--- a/solution.py
+++ b/solution.py
@@ -50,7 +50,7 @@
     return high, (value - high.astype(F32)).astype(BF16)
 
 
-def table_kernel(counts, dens, fock, nuclear, coords, table):
+def table_kernel(counts, dens, fock, nuclear, coords, table, packed, matrices):
     lane = iota((1, 128), 1)
     trace_sum = jnp.zeros((FRAG_DEV, 128), F32)
     diagonal = jnp.zeros((FRAG_DEV, 128), F32)
@@ -85,14 +85,51 @@
         value = jnp.where(row == index, content, value)
     for peer in range(N_FRAG):
         table[peer] = value
+    unflatten(fock, matrices)
+    pack_rows(matrices, packed)
+
+
+def pack_rows(matrices, packed):
+    lane = iota((8, 128), 1)
+
+    def row(index):
+        return matrices[8 * index : 8 * index + 8, :]
+
+    rows = [
+        jnp.where(lane < NB, row(index), pltpu.roll(row(64 + index), 32, 1)) for index in range(32)
+    ]
+    for index in range(16):
+        left, right = pltpu.roll(row(32 + index), 96, 1), pltpu.roll(row(48 + index), 32, 1)
+        rows.append(jnp.where(lane < 64, left, right))
+    for index in range(0, 48, 2):
+        both = jnp.concatenate(rows[index : index + 2], axis=0)
+        packed[8 * index : 8 * index + 16, :] = both.astype(BF16)
+
+
+def unpacked(rows):
+    lane = iota((32, 128), 1)
+    top, middle = rows[:32, :], rows[32:, :]
+    turned = jnp.concatenate([rows, jnp.zeros((80, 128), F32)], axis=0).T
+    first = jnp.where(lane < NB, top, 0.0)
+    beside = jnp.concatenate([pltpu.roll(middle, 32, 1), pltpu.roll(middle, 96, 1)], axis=0)
+    second = jnp.where(lane < 32, turned[32:64, :], jnp.where(lane < NB, beside, 0.0))
+    third = jnp.where(lane < NB, pltpu.roll(top, 96, 1), 0.0)
+    third = jnp.where(lane < 64, pltpu.roll(turned[96:128, :], 16, 1), third)
+    third = jnp.where(lane < 48, turned[32:64, :], third)
+    third = jnp.where(lane < 32, turned[64:96, :], third)
+    return jnp.concatenate([first, second, third], axis=0)
 
 
 def atom_table(density, fock_blocks, nuclear_charge, atom_counts, coords):
     return pl.pallas_call(
         table_kernel,
-        out_shape=jax.ShapeDtypeStruct((N_FRAG, 8, 128), F32),
+        out_shape=(
+            jax.ShapeDtypeStruct((N_FRAG, 8, 128), F32),
+            jax.ShapeDtypeStruct((48 * FRAG_DEV, 128), BF16),
+        ),
         in_specs=[pl.BlockSpec(memory_space=SMEM)] + [pl.BlockSpec(memory_space=VMEM)] * 4,
-        out_specs=pl.BlockSpec(memory_space=VMEM),
+        out_specs=(pl.BlockSpec(memory_space=VMEM),) * 2,
+        scratch_shapes=[VMEM((8 * NB, 128), F32)],
         name="atom_table",
     )(atom_counts, density, fock_blocks, nuclear_charge.reshape(1, 128), coords)
 
@@ -203,7 +240,7 @@
     fock_rows, shifted, state, high, low, square_high, square_low,
 ):
     for far, fock in enumerate((fock_0, fock_1, fock_2, fock_3)):
-        unflatten(fock, fock_rows.at[far])
+        fock_rows[far] = fock[...].astype(F32)
     base = (pairs[0, 0] // FRAG_DEV) * FRAG_DEV
     pair_base = (base // NA) * NA
     for buffer in (high, low, square_high, square_low):
@@ -216,7 +253,7 @@
     centres = []
     for dimer in range(DIM_DEV):
         held = pairs[dimer, 1] - base
-        part = fock_rows[held // FRAG_DEV, pl.ds(held % FRAG_DEV, NB, stride=8), :]
+        part = unpacked(fock_rows[held // FRAG_DEV, pl.ds(held % FRAG_DEV, 48, stride=8), :])
         shifted[dimer, :NB, :] = fixed[dimer, :NB, :]
         shifted[dimer, NB:, :128] = fixed[dimer, NB:, :128]
         shifted[dimer, NB:, 128:] = fixed[dimer, NB:, 128:] + part
@@ -295,7 +332,7 @@
         in_specs=[pl.BlockSpec(memory_space=SMEM)] + [pl.BlockSpec(memory_space=VMEM)] * 6,
         out_specs=(pl.BlockSpec(memory_space=VMEM), pl.BlockSpec(memory_space=SMEM)),
         scratch_shapes=[
-            VMEM((REACH + 1, 8 * NB, 128), F32),
+            VMEM((REACH + 1, 48 * FRAG_DEV, 128), F32),
             VMEM(matrix, F32),
             VMEM(matrix, F32),
             VMEM(split, BF16),
@@ -448,11 +485,11 @@
 
 
 def per_device(density, fock_blocks, coupling, dimer_pairs, atom_counts, nuclear_charge, coords):
-    table = atom_table(density, fock_blocks, nuclear_charge, atom_counts, coords)
-    focks = [fock_blocks]
+    table, packed = atom_table(density, fock_blocks, nuclear_charge, atom_counts, coords)
+    focks = [packed]
     for distance in range(1, REACH + 1):
         moves = [(index + distance, index) for index in range(N_FRAG - distance)]
-        focks.append(lax.ppermute(fock_blocks, FRAG, moves))
+        focks.append(lax.ppermute(packed, FRAG, moves))
     table = exchange(table, FRAG)
     fixed, starts = prepare_dimers(dimer_pairs, table, fock_blocks, coupling)
     sent, energies = solve_dimers(dimer_pairs, fixed, starts, focks)

time: 85.6 us -> 83.1 us (0.971)
  waiting for transfers between devices: 10.6 us -> 7.92 us
  starting transfers between devices: 27 us -> 25.2 us
  blocking collectives: 30.5 us -> 32.3 us
    ppermute x3, waiting for transfers between devices: 3.48 us -> 0.01 us  [per_device(): focks.append(lax.ppermute(packed, FRAG, moves))]
    all_to_all x2, blocking collectives: 30.5 us -> 32.3 us  [exchange(): return lax.all_to_all(value, axis, split_axis=0, concat_axis=0, tiled=True)]
  transfers between devices with their start and end apart: 7 -> 7, of which waited for: 3 -> 2; matrix products, arithmetic and copies ran while one was open for 0% -> 0% of each run, Pallas kernels for 3% -> 3%
where the time goes in v3:
time: 83.1 us; the launch traced here: 82.7 us
  blocking collectives  32.3 us (39%)
  starting transfers between devices  25.2 us (30%)
  Pallas kernels  16.4 us (20%)
  waiting for transfers between devices  7.92 us (10%)
    all_to_all x2, blocking collectives, exchange(): return lax.all_to_all(value, axis, split_axis=0, concat_axis=0, tiled=True)  32.3 us
    all_to_all x1, starting transfers between devices, exchange(): return lax.all_to_all(value, axis, split_axis=0, concat_axis=0, tiled=True)  11.3 us
    pallas_call x1, Pallas kernels, solve_dimers(): pl.pallas_call(solve_kernel, out_shape=(jax.ShapeDtypeStruct((N_TEAM * 32...  10.2 us
    ppermute x3, starting transfers between devices, per_device(): focks.append(lax.ppermute(packed, FRAG, moves))  4.73 us
    ppermute x1, starting transfers between devices, per_device(): lax.ppermute(next_2, PAIR, [(index, index + 2) for index in range(N_PAIR...  4.25 us
    all_to_all x1, waiting for transfers between devices, exchange(): return lax.all_to_all(value, axis, split_axis=0, concat_axis=0, tiled=True)  4.12 us
    ppermute x1, waiting for transfers between devices, per_device(): energy = lax.ppermute(energy, GRP_FRAG, energy_moves())  3.79 us
    pallas_call x1, Pallas kernels, prepare_dimers(): pl.pallas_call(prepare_kernel, out_shape=(jax.ShapeDtypeStruct((DIM_DEV,...  2.7 us
  transfers between devices with their start and end apart: 7, of which 2 were waited for; matrix products, arithmetic and copies ran while one was open for 0% of the time, Pallas kernels for 3%

profile of v3, /device:TPU:1, one launch (start us, length us, event | category | flops | bytes accessed | tf_op | source)
XLA Modules:
  0.0 82.7 jit_solution(1062506514399740836)
XLA Ops:
  0.6 0.0 copy-start.3
  0.6 2.0 %atom_table.1 = (f32[32,8,128]{2,1,0:T(8,128)}, bf16[384,128]{1,0:T(8,128)(2,1)}) custom-call(s32[8]{0:T(128)} %counts.1, bf16[8,9216]{1,0:T(8,128)(2,1)} %dens.3, bf16[8,9216]{1,0:T(8,128)(2,1)} %fock.3, f32[1,128]{1,0:T(1,128)} %bitcast.6, f32[3,128]{1,0:T(4,128)} %coords.1), custom_call_target="tpu_custom_call" | custom-call | tf_op jit(solution)/shard_map/atom_table/pallas_call | solution.py:124
  2.7 0.0 copy-start.1
  2.7 11.3 %all-to-all-start = ((f32[32,8,128]{2,1,0:T(8,128)}), f32[32,8,128]{2,1,0:T(8,128)S(1)}, u32[]{:S(2)}, u32[]{:S(2)}) async-start(f32[32,8,128]{2,1,0:T(8,128)} %get-tuple-element.15), calls=%async_computation | async-start | bytes 262144 | tf_op jit(solution)/shard_map/all_to_all | solution.py:41
  13.9 0.0 copy-start.4
  13.9 0.0 copy-done.2
  14.0 1.3 %collective-permute-start.2 = (bf16[384,128]{1,0:T(8,128)(2,1)S(1)}, bf16[384,128]{1,0:T(8,128)(2,1)S(1)}, u32[]{:S(2)}, u32[]{:S(2)}) collective-permute-start(bf16[384,128]{1,0:T(8,128)(2,1)S(1)} %copy-done.2), channel_id=1, source_target_pairs={{3,0},{4,1},{5,2},{6,3},{7,4},{8,5},{9,6},{10,7},{11,8},{12,9},{13... | collective-permute-start | bytes 294920 | tf_op jit(solution)/shard_map/ppermute | solution.py:492
  15.3 1.3 %collective-permute-start.1 = (bf16[384,128]{1,0:T(8,128)(2,1)S(1)}, bf16[384,128]{1,0:T(8,128)(2,1)S(1)}, u32[]{:S(2)}, u32[]{:S(2)}) collective-permute-start(bf16[384,128]{1,0:T(8,128)(2,1)S(1)} %copy-done.2), channel_id=1, source_target_pairs={{2,0},{3,1},{4,2},{5,3},{6,4},{7,5},{8,6},{9,7},{10,8},{11,9},{12,... | collective-permute-start | bytes 294920 | tf_op jit(solution)/shard_map/ppermute | solution.py:492
  16.6 2.1 %collective-permute-start = (bf16[384,128]{1,0:T(8,128)(2,1)S(1)}, bf16[384,128]{1,0:T(8,128)(2,1)S(1)}, u32[]{:S(2)}, u32[]{:S(2)}) collective-permute-start(bf16[384,128]{1,0:T(8,128)(2,1)S(1)} %copy-done.2), channel_id=1, source_target_pairs={{1,0},{2,1},{3,2},{4,3},{5,4},{6,5},{7,6},{8,7},{9,8},{10,9},{11,1... | collective-permute-start | bytes 294920 | tf_op jit(solution)/shard_map/ppermute | solution.py:492
  18.7 0.0 copy-done.4
  18.7 0.1 copy.11.pairs
  18.8 4.1 %all-to-all-done.table = f32[32,8,128]{2,1,0:T(8,128)S(1)} async-done(((f32[32,8,128]{2,1,0:T(8,128)}), f32[32,8,128]{2,1,0:T(8,128)S(1)}, u32[]{:S(2)}, u32[]{:S(2)}) %all-to-all-start) | async-done | bytes 131104 | tf_op jit(solution)/shard_map/all_to_all | solution.py:41
  22.9 0.0 copy-done.3
  22.9 0.0 copy-done.1
  22.9 2.7 %prepare_dimers.1 = (f32[4,192,256]{2,1,0:T(8,128)S(1)}, f32[8,128]{1,0:T(8,128)S(1)}) custom-call(s32[4,2]{1,0:T(4,128)S(1)} %copy.11.pairs, f32[32,8,128]{2,1,0:T(8,128)S(1)} %all-to-all-done.table, bf16[8,9216]{1,0:T(8,128)(2,1)S(1)} %copy-done.1, bf16[4,9216]{1,0:T(4,128)(2,1)S(1)} %copy-done.3), custom_call_target="tpu_custom_call" | custom-call | tf_op jit(solution)/shard_map/prepare_dimers/pallas_call | solution.py:219
  25.6 0.0 collective-permute-done.2.fock_3
  25.6 0.0 collective-permute-done.1.fock_2
  25.6 0.0 collective-permute-done.fock_1
  25.6 10.2 %solve_dimers.1 = (f32[512,128]{1,0:T(8,128)S(1)}, f32[4]{0:T(128)}) custom-call(s32[4,2]{1,0:T(4,128)S(1)} %copy.11.pairs, f32[4,192,256]{2,1,0:T(8,128)S(1)} %get-tuple-element.16.fixed, f32[8,128]{1,0:T(8,128)S(1)} %get-tuple-element.17.starts, bf16[384,128]{1,0:T(8,128)(2,1)S(1)} %copy-done.2, bf16[384,128]{1,0:T(8,128)(2,1)S(1)} %collective-permute-done.fock_1, ...), custom_call_target="tpu_custom_call" | custom-call | tf_op jit(solution)/shard_map/solve_dimers/pallas_call | solution.py:326
  35.8 16.8 %all_to_all.15.arrived = f32[16,32,128]{2,1,0:T(8,128)S(1)} all-to-all(f32[16,32,128]{2,1,0:T(8,128)S(1)} %bitcast.5), channel_id=1, replica_groups=mesh['grp_0'=2,'grp_1'=4,'frag_0'=2,'frag_1'=8,'frag_2'=2] {'grp_0','grp..., dimensions={0} | all-to-all | bytes 524288 | tf_op jit(solution)/shard_map/all_to_all | solution.py:41
  52.6 0.3 sort_blocks.1
  52.9 2.3 %collective-permute-start.3 = (bf16[16,512]{1,0:T(8,128)(2,1)S(1)}, bf16[16,512]{1,0:T(8,128)(2,1)S(1)}, u32[]{:S(2)}, u32[]{:S(2)}) collective-permute-start(bf16[16,512]{1,0:T(8,128)(2,1)S(1)} %get-tuple-element.21), channel_id=1, source_target_pairs={{0,2},{2,4},{4,6},{6,8},{8,10},{10,12},{12,14},{14,16},{16,18},{18... | collective-permute-start | bytes 49160 | tf_op jit(solution)/shard_map/ppermute | solution.py:498
  55.2 4.2 %collective-permute-start.4 = (bf16[16,512]{1,0:T(8,128)(2,1)S(1)}, bf16[16,512]{1,0:T(8,128)(2,1)S(1)}, u32[]{:S(2)}, u32[]{:S(2)}) collective-permute-start(bf16[16,512]{1,0:T(8,128)(2,1)S(1)} %get-tuple-element.22), channel_id=1, source_target_pairs={{0,4},{2,6},{4,8},{6,10},{8,12},{10,14},{12,16},{14,18},{16,20},{1... | collective-permute-start | bytes 49160 | tf_op jit(solution)/shard_map/ppermute | solution.py:499
  59.5 2.7 %collective-permute-start.5 = (f32[8,128]{1,0:T(8,128)S(1)}, f32[8,128]{1,0:T(8,128)S(1)}, u32[]{:S(2)}, u32[]{:S(2)}) collective-permute-start(f32[8,128]{1,0:T(8,128)S(1)} %get-tuple-element.23), channel_id=1, source_target_pairs={{0,0},{1,3},{2,2},{3,5},{4,4},{5,7},{6,6},{7,9},{8,8},{9,11},{10,1... | collective-permute-start | bytes 12296 | tf_op jit(solution)/shard_map/ppermute | solution.py:500
  62.2 3.8 %collective-permute-done.5.energy = f32[8,128]{1,0:T(8,128)S(1)} collective-permute-done((f32[8,128]{1,0:T(8,128)S(1)}, f32[8,128]{1,0:T(8,128)S(1)}, u32[]{:S(2)}, u32[]{:S(2)}) %collective-permute-start.5) | collective-permute-done | bytes 4128 | tf_op jit(solution)/shard_map/ppermute | solution.py:500
  66.0 0.0 collective-permute-done.3.from_1
  66.0 0.0 collective-permute-done.4.from_2
  66.0 0.1 join_blocks.1
  66.1 0.0 copy-start
  66.1 15.5 %all_to_all.16 = f32[16,32,128]{2,1,0:T(8,128)S(1)} all-to-all(f32[16,32,128]{2,1,0:T(8,128)S(1)} %join_blocks.1), channel_id=1, replica_groups=mesh['grp_0'=2,'grp_1'=4,'frag_0'=2,'frag_1'=8,'frag_2'=2] {'grp_0','grp..., dimensions={0} | all-to-all | bytes 524288 | tf_op jit(solution)/shard_map/all_to_all | solution.py:41
  81.6 0.0 copy-done
  81.6 1.1 %unpack_blocks.1 = (f32[8,9216]{1,0:T(8,128)}, f32[1,1]{1,0:T(1,128)}) custom-call(f32[512,128]{1,0:T(8,128)S(1)} %bitcast.4, bf16[8,9216]{1,0:T(8,128)(2,1)S(1)} %copy-done), custom_call_target="tpu_custom_call" | custom-call | tf_op jit(solution)/shard_map/unpack_blocks/pallas_call | solution.py:462
  (1 shorter events, 0.0 us)
Async XLA Ops:
  0.6 22.3 %copy-start.3 = (bf16[4,9216]{1,0:T(4,128)(2,1)S(1)}, bf16[4,9216]{1,0:T(4,128)(2,1)}, u32[]{:S(2)}) copy-start(bf16[4,9216]{1,0:T(4,128)(2,1)} %coupling.1) | copy-start | bytes 221188
  2.7 20.3 %copy-start.1 = (bf16[8,9216]{1,0:T(8,128)(2,1)S(1)}, bf16[8,9216]{1,0:T(8,128)(2,1)}, u32[]{:S(2)}) copy-start(bf16[8,9216]{1,0:T(8,128)(2,1)} %fock.3) | copy-start | bytes 442372
  2.7 11.3 %copy-start.2 = (bf16[384,128]{1,0:T(8,128)(2,1)S(1)}, bf16[384,128]{1,0:T(8,128)(2,1)}, u32[]{:S(2)}) copy-start(bf16[384,128]{1,0:T(8,128)(2,1)} %get-tuple-element.18.fock_0) | copy-start | bytes 294916
  2.7 20.3 %all-to-all-start = ((f32[32,8,128]{2,1,0:T(8,128)}), f32[32,8,128]{2,1,0:T(8,128)S(1)}, u32[]{:S(2)}, u32[]{:S(2)}) async-start(f32[32,8,128]{2,1,0:T(8,128)} %get-tuple-element.15), calls=%async_computation | async-start | bytes 262144 | tf_op jit(solution)/shard_map/all_to_all | solution.py:41
  13.9 4.8 %copy-start.4 = (s32[4,2]{0,1:T(2,128)S(1)}, s32[4,2]{0,1:T(2,128)}, u32[]{:S(2)}) copy-start(s32[4,2]{0,1:T(2,128)} %param.10) | copy-start | bytes 100
  14.0 11.7 %collective-permute-start.2 = (bf16[384,128]{1,0:T(8,128)(2,1)S(1)}, bf16[384,128]{1,0:T(8,128)(2,1)S(1)}, u32[]{:S(2)}, u32[]{:S(2)}) collective-permute-start(bf16[384,128]{1,0:T(8,128)(2,1)S(1)} %copy-done.2), channel_id=1, source_target_pairs={{3,0},{4,1},{5,2},{6,3},{7,4},{8,5},{9,6},{10,7},{11,8},{12,9},{13... | collective-permute-start | bytes 294920 | tf_op jit(solution)/shard_map/ppermute | solution.py:492
  15.3 10.4 %collective-permute-start.1 = (bf16[384,128]{1,0:T(8,128)(2,1)S(1)}, bf16[384,128]{1,0:T(8,128)(2,1)S(1)}, u32[]{:S(2)}, u32[]{:S(2)}) collective-permute-start(bf16[384,128]{1,0:T(8,128)(2,1)S(1)} %copy-done.2), channel_id=1, source_target_pairs={{2,0},{3,1},{4,2},{5,3},{6,4},{7,5},{8,6},{9,7},{10,8},{11,9},{12,... | collective-permute-start | bytes 294920 | tf_op jit(solution)/shard_map/ppermute | solution.py:492
  16.6 9.1 %collective-permute-start = (bf16[384,128]{1,0:T(8,128)(2,1)S(1)}, bf16[384,128]{1,0:T(8,128)(2,1)S(1)}, u32[]{:S(2)}, u32[]{:S(2)}) collective-permute-start(bf16[384,128]{1,0:T(8,128)(2,1)S(1)} %copy-done.2), channel_id=1, source_target_pairs={{1,0},{2,1},{3,2},{4,3},{5,4},{6,5},{7,6},{8,7},{9,8},{10,9},{11,1... | collective-permute-start | bytes 294920 | tf_op jit(solution)/shard_map/ppermute | solution.py:492
  52.9 13.0 %collective-permute-start.3 = (bf16[16,512]{1,0:T(8,128)(2,1)S(1)}, bf16[16,512]{1,0:T(8,128)(2,1)S(1)}, u32[]{:S(2)}, u32[]{:S(2)}) collective-permute-start(bf16[16,512]{1,0:T(8,128)(2,1)S(1)} %get-tuple-element.21), channel_id=1, source_target_pairs={{0,2},{2,4},{4,6},{6,8},{8,10},{10,12},{12,14},{14,16},{16,18},{18... | collective-permute-start | bytes 49160 | tf_op jit(solution)/shard_map/ppermute | solution.py:498
  55.2 10.7 %collective-permute-start.4 = (bf16[16,512]{1,0:T(8,128)(2,1)S(1)}, bf16[16,512]{1,0:T(8,128)(2,1)S(1)}, u32[]{:S(2)}, u32[]{:S(2)}) collective-permute-start(bf16[16,512]{1,0:T(8,128)(2,1)S(1)} %get-tuple-element.22), channel_id=1, source_target_pairs={{0,4},{2,6},{4,8},{6,10},{8,12},{10,14},{12,16},{14,18},{16,20},{1... | collective-permute-start | bytes 49160 | tf_op jit(solution)/shard_map/ppermute | solution.py:499
  59.5 6.5 %collective-permute-start.5 = (f32[8,128]{1,0:T(8,128)S(1)}, f32[8,128]{1,0:T(8,128)S(1)}, u32[]{:S(2)}, u32[]{:S(2)}) collective-permute-start(f32[8,128]{1,0:T(8,128)S(1)} %get-tuple-element.23), channel_id=1, source_target_pairs={{0,0},{1,3},{2,2},{3,5},{4,4},{5,7},{6,6},{7,9},{8,8},{9,11},{10,1... | collective-permute-start | bytes 12296 | tf_op jit(solution)/shard_map/ppermute | solution.py:500
  66.1 15.5 %copy-start = (bf16[8,9216]{1,0:T(8,128)(2,1)S(1)}, bf16[8,9216]{1,0:T(8,128)(2,1)}, u32[]{:S(2)}) copy-start(bf16[8,9216]{1,0:T(8,128)(2,1)} %dens.3) | copy-start | bytes 442372

commit v4 on v3

--- a/solution.py
+++ b/solution.py
@@ -11,6 +11,7 @@
 REACH = 3
 PURIF = 12
 UNROLL = 6
+BATCH = 8
 FRAG_DEV = 8
 DIM_DEV = 4
 FLAT = NB * NB
@@ -27,10 +28,11 @@
 VMEM = pltpu.VMEM
 SMEM = pltpu.SMEM
 
-ID_LANE = 96
-ONE_LANE = 97
-ENERGY_LANE = 98
-SUM_LANE = 99
+PARTS = 3
+ID_LANE = 64
+ONE_LANE = 65
+ENERGY_LANE = 66
+SUM_LANE = 67
 
 
 def iota(shape, dim):
@@ -113,6 +115,8 @@
     first = jnp.where(lane < NB, top, 0.0)
     beside = jnp.concatenate([pltpu.roll(middle, 32, 1), pltpu.roll(middle, 96, 1)], axis=0)
     second = jnp.where(lane < 32, turned[32:64, :], jnp.where(lane < NB, beside, 0.0))
+    mirrored = jnp.logical_and(iota((32, 128), 0) >= 16, jnp.logical_and(lane >= 32, lane < 48))
+    second = jnp.where(mirrored, turned[:32, :], second)
     third = jnp.where(lane < NB, pltpu.roll(top, 96, 1), 0.0)
     third = jnp.where(lane < 64, pltpu.roll(turned[96:128, :], 16, 1), third)
     third = jnp.where(lane < 48, turned[32:64, :], third)
@@ -181,8 +185,8 @@
 
         def gather(step, sums, dimer=dimer, places=places):
             sums = list(sums)
-            for inner in range(4):
-                block = step * 4 + inner
+            for inner in range(BATCH):
+                block = step * BATCH + inner
                 weight = masked[dimer, pl.ds(block, 1), :]
                 spot = [table[block, k : k + 1, :] for k in (1, 2, 3)]
                 for side in range(2):
@@ -192,7 +196,7 @@
             return tuple(sums)
 
         zero = jnp.zeros((NA, 128), F32)
-        sums = lax.fori_loop(0, N_FRAG // 4, gather, (zero, zero))
+        sums = lax.fori_loop(0, N_FRAG // BATCH, gather, (zero, zero))
         start = jnp.zeros((1, 1), F32)
         for side in range(2):
             potential = jnp.sum(sums[side], axis=1, keepdims=True)
@@ -288,21 +292,24 @@
         trace = jnp.sum(jnp.where(eye, final, 0.0), axis=(0, 1), keepdims=True)
         centre = centres[dimer]
         energy = 0.5 * (2.0 * NB * centre - overlap - centre * trace) - starts[dimer : dimer + 1, 0:1]
-        energies[dimer] = jnp.sum(energy)
+        energies[dimer : dimer + 1, :] = jnp.broadcast_to(energy, (1, 128))
         for side in range(2):
             slot = side * DIM_DEV + dimer
             block = final[side * NB : (side + 1) * NB, side * 128 : (side + 1) * 128]
+            target = (pairs[dimer, side] - pair_base).astype(F32)
             corner = pltpu.roll(block[64:96, :], 32, 1)
-            target = (pairs[dimer, side] - pair_base).astype(F32)
-            beside = jnp.where(lane_16 == ID_LANE, target, 0.0)
-            beside = jnp.where(lane_16 == ONE_LANE, 1.0, beside)
-            if side == 0:
-                beside = jnp.where(lane_16 == ENERGY_LANE, energy, beside)
-            for part in range(4):
-                piece = block[16 * part : 16 * (part + 1), :]
-                other = corner[16 * part : 16 * (part + 1), :] if part < 2 else beside
-                piece = jnp.where(lane_16 < NB, piece, other)
-                sent[pl.ds(part * 8 + slot, 16, stride=32), :] = piece
+            pieces = [
+                jnp.where(lane_16 < NB, block[:16, :], corner[:16, :]),
+                jnp.where(lane_16 < NB, block[16:32, :], corner[16:, :]),
+            ]
+            left, right = pltpu.roll(block[32:48, :], 96, 1), pltpu.roll(block[48:64, :], 32, 1)
+            piece = jnp.where(lane_16 < 64, left, right)
+            piece = jnp.where(lane_16 == ID_LANE, target, piece)
+            piece = jnp.where(lane_16 == ONE_LANE, 1.0, piece)
+            beside = energy if side == 0 else jnp.zeros((1, 1), F32)
+            pieces.append(jnp.where(lane_16 == ENERGY_LANE, beside, piece))
+            for part, piece in enumerate(pieces):
+                sent[pl.ds(part * 8 + slot, 16, stride=8 * PARTS), :] = piece
 
 
 def keep(high, low, dimer, value):
@@ -326,11 +333,11 @@
     return pl.pallas_call(
         solve_kernel,
         out_shape=(
-            jax.ShapeDtypeStruct((N_TEAM * 32, 128), F32),
-            jax.ShapeDtypeStruct((DIM_DEV,), F32),
+            jax.ShapeDtypeStruct((N_TEAM * 8 * PARTS, 128), F32),
+            jax.ShapeDtypeStruct((8, 128), F32),
         ),
         in_specs=[pl.BlockSpec(memory_space=SMEM)] + [pl.BlockSpec(memory_space=VMEM)] * 6,
-        out_specs=(pl.BlockSpec(memory_space=VMEM), pl.BlockSpec(memory_space=SMEM)),
+        out_specs=(pl.BlockSpec(memory_space=VMEM),) * 2,
         scratch_shapes=[
             VMEM((REACH + 1, 48 * FRAG_DEV, 128), F32),
             VMEM(matrix, F32),
@@ -347,7 +354,7 @@
 
 def sort_kernel(arrived, own, next_1, next_2, energy):
     parts = [
-        arrived[:, part * 8 : (part + 1) * 8, :].reshape(N_TEAM * 8, 128) for part in range(4)
+        arrived[:, part * 8 : (part + 1) * 8, :].reshape(N_TEAM * 8, 128) for part in range(PARTS)
     ]
     target = parts[2][:, ID_LANE : ID_LANE + 1].astype(jnp.int32)
     chosen = jnp.where(iota((128, 64), 1) == target, 1.0, 0.0).astype(BF16)
@@ -356,7 +363,7 @@
     rest = value - upper.astype(F32)
     middle = rest.astype(BF16)
     lower = (rest - middle.astype(F32)).astype(BF16)
-    total = jnp.zeros((64, 512), F32)
+    total = jnp.zeros((64, 128 * PARTS), F32)
     for piece in (lower, middle, upper):
         total += lax.dot_general(
             chosen, piece, (((0,), (0,)), ((), ())), preferred_element_type=F32
@@ -372,9 +379,9 @@
     return pl.pallas_call(
         sort_kernel,
         out_shape=(
-            jax.ShapeDtypeStruct((16, 512), F32),
-            jax.ShapeDtypeStruct((16, 512), BF16),
-            jax.ShapeDtypeStruct((16, 512), BF16),
+            jax.ShapeDtypeStruct((16, 128 * PARTS), F32),
+            jax.ShapeDtypeStruct((16, 128 * PARTS), BF16),
+            jax.ShapeDtypeStruct((16, 128 * PARTS), BF16),
             jax.ShapeDtypeStruct((8, 128), F32),
         ),
         in_specs=[pl.BlockSpec(memory_space=VMEM)],
@@ -389,7 +396,7 @@
     lane = iota((8, 128), 1)
     mine = jnp.broadcast_to(energy[0:1, ENERGY_LANE : ENERGY_LANE + 1], (8, 128))
     for core in range(2):
-        for part in range(4):
+        for part in range(PARTS):
             rows = total[core * 8 : core * 8 + 8, part * 128 : (part + 1) * 128]
             if part == 2:
                 rows = jnp.where(lane == SUM_LANE, mine, rows)
@@ -400,7 +407,7 @@
 def join_blocks(own, from_1, from_2, energy):
     return pl.pallas_call(
         join_kernel,
-        out_shape=jax.ShapeDtypeStruct((N_TEAM, 32, 128), F32),
+        out_shape=jax.ShapeDtypeStruct((N_TEAM, 8 * PARTS, 128), F32),
         in_specs=[pl.BlockSpec(memory_space=VMEM)] * 4,
         out_specs=pl.BlockSpec(memory_space=VMEM),
         compiler_params=pltpu.CompilerParams(vmem_limit_bytes=4 << 20),
@@ -408,33 +415,21 @@
     )(own, from_1, from_2, energy)
 
 
-def unpack_kernel(arrived, dens, out, total, turned):
+def unpack_kernel(arrived, dens, energy_rows, out, total, energies, turned):
+    for dimer in range(DIM_DEV):
+        energies[dimer] = jnp.sum(energy_rows[dimer : dimer + 1, 0:1])
     for fragment in range(FRAG_DEV):
-        upper = jnp.concatenate(
-            [
-                arrived[pl.ds(part * 8 + fragment, 16, stride=32), :]
-                for part in range(4)
-            ],
-            axis=0,
-        )
-        turned[pl.ds(fragment, 32, stride=8), :] = jnp.concatenate(
-            [upper.T[64:96, :], jnp.zeros((32, 64), F32)], axis=1
-        )
+        rows = [
+            arrived[pl.ds(part * 8 + fragment, 16, stride=8 * PARTS), :] for part in range(PARTS)
+        ]
+        turned[pl.ds(fragment, NB, stride=8), :] = unpacked(jnp.concatenate(rows, axis=0))
     lane = iota((8, 128), 1)
     number = arrived[16:24, ONE_LANE : ONE_LANE + 1]
     number = jnp.broadcast_to(number, (8, 128))
     half_number = 0.5 * number
 
-    def packed(row):
-        start = (row % 16) * 32 + (row // 16) * 8
-        return arrived[start : start + 8, :]
-
     def matrix_row(row):
-        if row < 64:
-            return packed(row)
-        left = turned[(row - 64) * 8 : (row - 64) * 8 + 8, :]
-        right = pltpu.roll(packed(row - 64), 96, 1)
-        return jnp.where(lane < 64, left, right)
+        return turned[row * 8 : row * 8 + 8, :]
 
     def finish(tile, value):
         here = slice(tile * 128, (tile + 1) * 128)
@@ -454,23 +449,29 @@
 
     energy = jnp.zeros((1, 128), F32)
     for member in range(N_TEAM):
-        energy += arrived[member * 32 + 16 : member * 32 + 17, :]
-    total[...] = energy[:, SUM_LANE : SUM_LANE + 1]
-
-
-def unpack_blocks(arrived, density):
+        start = member * 8 * PARTS + 16
+        energy += arrived[start : start + 1, :]
+    total[0] = jnp.sum(energy[:, SUM_LANE : SUM_LANE + 1])
+
+
+def unpack_blocks(arrived, density, energies):
     return pl.pallas_call(
         unpack_kernel,
         out_shape=(
             jax.ShapeDtypeStruct((FRAG_DEV, FLAT), F32),
-            jax.ShapeDtypeStruct((1, 1), F32),
-        ),
-        in_specs=[pl.BlockSpec(memory_space=VMEM)] * 2,
-        out_specs=(pl.BlockSpec(memory_space=VMEM),) * 2,
-        scratch_shapes=[VMEM((256, 128), F32)],
+            jax.ShapeDtypeStruct((1,), F32),
+            jax.ShapeDtypeStruct((DIM_DEV,), F32),
+        ),
+        in_specs=[pl.BlockSpec(memory_space=VMEM)] * 3,
+        out_specs=(
+            pl.BlockSpec(memory_space=VMEM),
+            pl.BlockSpec(memory_space=SMEM),
+            pl.BlockSpec(memory_space=SMEM),
+        ),
+        scratch_shapes=[VMEM((8 * NB, 128), F32)],
         compiler_params=pltpu.CompilerParams(vmem_limit_bytes=4 << 20),
         name="unpack_blocks",
-    )(arrived.reshape(N_TEAM * 32, 128), density)
+    )(arrived.reshape(N_TEAM * 8 * PARTS, 128), density, energies)
 
 
 def energy_moves():
@@ -493,13 +494,13 @@
     table = exchange(table, FRAG)
     fixed, starts = prepare_dimers(dimer_pairs, table, fock_blocks, coupling)
     sent, energies = solve_dimers(dimer_pairs, fixed, starts, focks)
-    arrived = exchange(sent.reshape(N_TEAM, 32, 128), TEAM)
+    arrived = exchange(sent.reshape(N_TEAM, 8 * PARTS, 128), TEAM)
     own, next_1, next_2, energy = sort_blocks(arrived)
     from_1 = lax.ppermute(next_1, PAIR, [(index, index + 1) for index in range(N_PAIR - 1)])
     from_2 = lax.ppermute(next_2, PAIR, [(index, index + 2) for index in range(N_PAIR - 2)])
     energy = lax.ppermute(energy, GRP_FRAG, energy_moves())
     arrived = exchange(join_blocks(own, from_1, from_2, energy), TEAM)
-    correction, total = unpack_blocks(arrived, density)
+    correction, total, energies = unpack_blocks(arrived, density, energies)
     return correction, energies, total.reshape(())
 
 

time: 83.1 us -> 81.5 us (0.981)
  blocking collectives: 32.3 us -> 31.2 us
    all_to_all x2, blocking collectives: 32.3 us -> 31.2 us  [exchange(): return lax.all_to_all(value, axis, split_axis=0, concat_axis=0, tiled=True)]
where the time goes in v4:
time: 81.5 us; the launch traced here: 81.1 us
  blocking collectives  31.2 us (38%)
  starting transfers between devices  25.3 us (31%)
  Pallas kernels  15.8 us (19%)
  waiting for transfers between devices  7.92 us (10%)
    all_to_all x2, blocking collectives, exchange(): return lax.all_to_all(value, axis, split_axis=0, concat_axis=0, tiled=True)  31.2 us
    all_to_all x1, starting transfers between devices, exchange(): return lax.all_to_all(value, axis, split_axis=0, concat_axis=0, tiled=True)  11.3 us
    pallas_call x1, Pallas kernels, solve_dimers(): pl.pallas_call(solve_kernel, out_shape=(jax.ShapeDtypeStruct((N_TEAM * 8...  9.58 us
    ppermute x3, starting transfers between devices, per_device(): focks.append(lax.ppermute(packed, FRAG, moves))  4.73 us
    ppermute x1, starting transfers between devices, per_device(): lax.ppermute(next_2, PAIR, [(index, index + 2) for index in range(N_PAIR...  4.35 us
    all_to_all x1, waiting for transfers between devices, exchange(): return lax.all_to_all(value, axis, split_axis=0, concat_axis=0, tiled=True)  4.12 us
    ppermute x1, waiting for transfers between devices, per_device(): energy = lax.ppermute(energy, GRP_FRAG, energy_moves())  3.79 us
    ppermute x1, starting transfers between devices, per_device(): energy = lax.ppermute(energy, GRP_FRAG, energy_moves())  2.67 us
  transfers between devices with their start and end apart: 7, of which 2 were waited for; matrix products, arithmetic and copies ran while one was open for 0% of the time, Pallas kernels for 3%

profile of v4, /device:TPU:1, one launch (start us, length us, event | category | flops | bytes accessed | tf_op | source)
XLA Modules:
  0.0 81.1 jit_solution(13620227284388450396)
XLA Ops:
  0.6 0.0 copy-start.3
  0.6 2.0 %atom_table.1 = (f32[32,8,128]{2,1,0:T(8,128)}, bf16[384,128]{1,0:T(8,128)(2,1)}) custom-call(s32[8]{0:T(128)} %counts.1, bf16[8,9216]{1,0:T(8,128)(2,1)} %dens.3, bf16[8,9216]{1,0:T(8,128)(2,1)} %fock.3, f32[1,128]{1,0:T(1,128)} %bitcast.6, f32[3,128]{1,0:T(4,128)} %coords.1), custom_call_target="tpu_custom_call" | custom-call | tf_op jit(solution)/shard_map/atom_table/pallas_call | solution.py:128
  2.7 0.0 copy-start
  2.7 11.3 %all-to-all-start = ((f32[32,8,128]{2,1,0:T(8,128)}), f32[32,8,128]{2,1,0:T(8,128)S(1)}, u32[]{:S(2)}, u32[]{:S(2)}) async-start(f32[32,8,128]{2,1,0:T(8,128)} %get-tuple-element.16), calls=%async_computation | async-start | bytes 262144 | tf_op jit(solution)/shard_map/all_to_all | solution.py:43
  13.9 0.0 copy-start.4
  13.9 0.0 copy-done.2
  13.9 1.3 %collective-permute-start.2 = (bf16[384,128]{1,0:T(8,128)(2,1)S(1)}, bf16[384,128]{1,0:T(8,128)(2,1)S(1)}, u32[]{:S(2)}, u32[]{:S(2)}) collective-permute-start(bf16[384,128]{1,0:T(8,128)(2,1)S(1)} %copy-done.2), channel_id=1, source_target_pairs={{3,0},{4,1},{5,2},{6,3},{7,4},{8,5},{9,6},{10,7},{11,8},{12,9},{13... | collective-permute-start | bytes 294920 | tf_op jit(solution)/shard_map/ppermute | solution.py:493
  15.2 1.3 %collective-permute-start.1 = (bf16[384,128]{1,0:T(8,128)(2,1)S(1)}, bf16[384,128]{1,0:T(8,128)(2,1)S(1)}, u32[]{:S(2)}, u32[]{:S(2)}) collective-permute-start(bf16[384,128]{1,0:T(8,128)(2,1)S(1)} %copy-done.2), channel_id=1, source_target_pairs={{2,0},{3,1},{4,2},{5,3},{6,4},{7,5},{8,6},{9,7},{10,8},{11,9},{12,... | collective-permute-start | bytes 294920 | tf_op jit(solution)/shard_map/ppermute | solution.py:493
  16.5 2.1 %collective-permute-start = (bf16[384,128]{1,0:T(8,128)(2,1)S(1)}, bf16[384,128]{1,0:T(8,128)(2,1)S(1)}, u32[]{:S(2)}, u32[]{:S(2)}) collective-permute-start(bf16[384,128]{1,0:T(8,128)(2,1)S(1)} %copy-done.2), channel_id=1, source_target_pairs={{1,0},{2,1},{3,2},{4,3},{5,4},{6,5},{7,6},{8,7},{9,8},{10,9},{11,1... | collective-permute-start | bytes 294920 | tf_op jit(solution)/shard_map/ppermute | solution.py:493
  18.7 0.0 copy-done.4
  18.7 0.1 copy.11.pairs
  18.8 4.1 %all-to-all-done.table = f32[32,8,128]{2,1,0:T(8,128)S(1)} async-done(((f32[32,8,128]{2,1,0:T(8,128)}), f32[32,8,128]{2,1,0:T(8,128)S(1)}, u32[]{:S(2)}, u32[]{:S(2)}) %all-to-all-start) | async-done | bytes 131104 | tf_op jit(solution)/shard_map/all_to_all | solution.py:43
  22.9 0.0 copy-done.3
  22.9 0.0 copy-done
  22.9 2.6 %prepare_dimers.1 = (f32[4,192,256]{2,1,0:T(8,128)S(1)}, f32[8,128]{1,0:T(8,128)S(1)}) custom-call(s32[4,2]{1,0:T(4,128)S(1)} %copy.11.pairs, f32[32,8,128]{2,1,0:T(8,128)S(1)} %all-to-all-done.table, bf16[8,9216]{1,0:T(8,128)(2,1)S(1)} %copy-done, bf16[4,9216]{1,0:T(4,128)(2,1)S(1)} %copy-done.3), custom_call_target="tpu_custom_call" | custom-call | tf_op jit(solution)/shard_map/prepare_dimers/pallas_call | solution.py:223
  25.5 0.0 collective-permute-done.2.fock_3
  25.5 0.0 collective-permute-done.1.fock_2
  25.5 0.0 collective-permute-done.fock_1
  25.5 9.6 %solve_dimers.1 = (f32[384,128]{1,0:T(8,128)S(1)}, f32[8,128]{1,0:T(8,128)S(1)}) custom-call(s32[4,2]{1,0:T(4,128)S(1)} %copy.11.pairs, f32[4,192,256]{2,1,0:T(8,128)S(1)} %get-tuple-element.17.fixed, f32[8,128]{1,0:T(8,128)S(1)} %get-tuple-element.18.starts, bf16[384,128]{1,0:T(8,128)(2,1)S(1)} %copy-done.2, ...), custom_call_target="tpu_custom_call" | custom-call | tf_op jit(solution)/shard_map/solve_dimers/pallas_call | solution.py:333
  35.1 16.2 %all_to_all.15.arrived = f32[16,24,128]{2,1,0:T(8,128)S(1)} all-to-all(f32[16,24,128]{2,1,0:T(8,128)S(1)} %bitcast.5), channel_id=1, replica_groups=mesh['grp_0'=2,'grp_1'=4,'frag_0'=2,'frag_1'=8,'frag_2'=2] {'grp_0','grp..., dimensions={0} | all-to-all | bytes 393216 | tf_op jit(solution)/shard_map/all_to_all | solution.py:43
  51.4 0.3 sort_blocks.1
  51.7 2.3 %collective-permute-start.3 = (bf16[16,384]{1,0:T(8,128)(2,1)S(1)}, bf16[16,384]{1,0:T(8,128)(2,1)S(1)}, u32[]{:S(2)}, u32[]{:S(2)}) collective-permute-start(bf16[16,384]{1,0:T(8,128)(2,1)S(1)} %get-tuple-element.22), channel_id=1, source_target_pairs={{0,2},{2,4},{4,6},{6,8},{8,10},{10,12},{12,14},{14,16},{16,18},{18... | collective-permute-start | bytes 36872 | tf_op jit(solution)/shard_map/ppermute | solution.py:499
  54.0 4.3 %collective-permute-start.4 = (bf16[16,384]{1,0:T(8,128)(2,1)S(1)}, bf16[16,384]{1,0:T(8,128)(2,1)S(1)}, u32[]{:S(2)}, u32[]{:S(2)}) collective-permute-start(bf16[16,384]{1,0:T(8,128)(2,1)S(1)} %get-tuple-element.23), channel_id=1, source_target_pairs={{0,4},{2,6},{4,8},{6,10},{8,12},{10,14},{12,16},{14,18},{16,20},{1... | collective-permute-start | bytes 36872 | tf_op jit(solution)/shard_map/ppermute | solution.py:500
  58.3 2.7 %collective-permute-start.5 = (f32[8,128]{1,0:T(8,128)S(1)}, f32[8,128]{1,0:T(8,128)S(1)}, u32[]{:S(2)}, u32[]{:S(2)}) collective-permute-start(f32[8,128]{1,0:T(8,128)S(1)} %get-tuple-element.24), channel_id=1, source_target_pairs={{0,0},{1,3},{2,2},{3,5},{4,4},{5,7},{6,6},{7,9},{8,8},{9,11},{10,1... | collective-permute-start | bytes 12296 | tf_op jit(solution)/shard_map/ppermute | solution.py:501
  61.0 3.8 %collective-permute-done.5.energy = f32[8,128]{1,0:T(8,128)S(1)} collective-permute-done((f32[8,128]{1,0:T(8,128)S(1)}, f32[8,128]{1,0:T(8,128)S(1)}, u32[]{:S(2)}, u32[]{:S(2)}) %collective-permute-start.5) | collective-permute-done | bytes 4128 | tf_op jit(solution)/shard_map/ppermute | solution.py:501
  64.8 0.0 collective-permute-done.3.from_1
  64.8 0.0 collective-permute-done.4.from_2
  64.8 0.1 join_blocks.1
  64.9 0.0 copy-start.1
  64.9 15.0 %all_to_all.16 = f32[16,24,128]{2,1,0:T(8,128)S(1)} all-to-all(f32[16,24,128]{2,1,0:T(8,128)S(1)} %join_blocks.1), channel_id=1, replica_groups=mesh['grp_0'=2,'grp_1'=4,'frag_0'=2,'frag_1'=8,'frag_2'=2] {'grp_0','grp..., dimensions={0} | all-to-all | bytes 393216 | tf_op jit(solution)/shard_map/all_to_all | solution.py:43
  79.9 0.0 copy-done.1
  79.9 1.2 %unpack_blocks.1 = (f32[8,9216]{1,0:T(8,128)}, f32[1]{0:T(128)}, f32[4]{0:T(128)}) custom-call(f32[384,128]{1,0:T(8,128)S(1)} %bitcast.4, bf16[8,9216]{1,0:T(8,128)(2,1)S(1)} %copy-done.1, f32[8,128]{1,0:T(8,128)S(1)} %get-tuple-element.25.energy_rows), custom_call_target="tpu_custom_call" | custom-call | tf_op jit(solution)/shard_map/unpack_blocks/pallas_call | solution.py:458
  (1 shorter events, 0.0 us)
Async XLA Ops:
  0.6 22.3 %copy-start.3 = (bf16[4,9216]{1,0:T(4,128)(2,1)S(1)}, bf16[4,9216]{1,0:T(4,128)(2,1)}, u32[]{:S(2)}) copy-start(bf16[4,9216]{1,0:T(4,128)(2,1)} %coupling.1) | copy-start | bytes 221188
  2.7 20.3 %copy-start = (bf16[8,9216]{1,0:T(8,128)(2,1)S(1)}, bf16[8,9216]{1,0:T(8,128)(2,1)}, u32[]{:S(2)}) copy-start(bf16[8,9216]{1,0:T(8,128)(2,1)} %fock.3) | copy-start | bytes 442372
  2.7 11.3 %copy-start.2 = (bf16[384,128]{1,0:T(8,128)(2,1)S(1)}, bf16[384,128]{1,0:T(8,128)(2,1)}, u32[]{:S(2)}) copy-start(bf16[384,128]{1,0:T(8,128)(2,1)} %get-tuple-element.19.fock_0) | copy-start | bytes 294916
  2.7 20.3 %all-to-all-start = ((f32[32,8,128]{2,1,0:T(8,128)}), f32[32,8,128]{2,1,0:T(8,128)S(1)}, u32[]{:S(2)}, u32[]{:S(2)}) async-start(f32[32,8,128]{2,1,0:T(8,128)} %get-tuple-element.16), calls=%async_computation | async-start | bytes 262144 | tf_op jit(solution)/shard_map/all_to_all | solution.py:43
  13.9 4.8 %copy-start.4 = (s32[4,2]{0,1:T(2,128)S(1)}, s32[4,2]{0,1:T(2,128)}, u32[]{:S(2)}) copy-start(s32[4,2]{0,1:T(2,128)} %param.10) | copy-start | bytes 100
  13.9 11.6 %collective-permute-start.2 = (bf16[384,128]{1,0:T(8,128)(2,1)S(1)}, bf16[384,128]{1,0:T(8,128)(2,1)S(1)}, u32[]{:S(2)}, u32[]{:S(2)}) collective-permute-start(bf16[384,128]{1,0:T(8,128)(2,1)S(1)} %copy-done.2), channel_id=1, source_target_pairs={{3,0},{4,1},{5,2},{6,3},{7,4},{8,5},{9,6},{10,7},{11,8},{12,9},{13... | collective-permute-start | bytes 294920 | tf_op jit(solution)/shard_map/ppermute | solution.py:493
  15.2 10.3 %collective-permute-start.1 = (bf16[384,128]{1,0:T(8,128)(2,1)S(1)}, bf16[384,128]{1,0:T(8,128)(2,1)S(1)}, u32[]{:S(2)}, u32[]{:S(2)}) collective-permute-start(bf16[384,128]{1,0:T(8,128)(2,1)S(1)} %copy-done.2), channel_id=1, source_target_pairs={{2,0},{3,1},{4,2},{5,3},{6,4},{7,5},{8,6},{9,7},{10,8},{11,9},{12,... | collective-permute-start | bytes 294920 | tf_op jit(solution)/shard_map/ppermute | solution.py:493
  16.5 9.0 %collective-permute-start = (bf16[384,128]{1,0:T(8,128)(2,1)S(1)}, bf16[384,128]{1,0:T(8,128)(2,1)S(1)}, u32[]{:S(2)}, u32[]{:S(2)}) collective-permute-start(bf16[384,128]{1,0:T(8,128)(2,1)S(1)} %copy-done.2), channel_id=1, source_target_pairs={{1,0},{2,1},{3,2},{4,3},{5,4},{6,5},{7,6},{8,7},{9,8},{10,9},{11,1... | collective-permute-start | bytes 294920 | tf_op jit(solution)/shard_map/ppermute | solution.py:493
  51.7 13.1 %collective-permute-start.3 = (bf16[16,384]{1,0:T(8,128)(2,1)S(1)}, bf16[16,384]{1,0:T(8,128)(2,1)S(1)}, u32[]{:S(2)}, u32[]{:S(2)}) collective-permute-start(bf16[16,384]{1,0:T(8,128)(2,1)S(1)} %get-tuple-element.22), channel_id=1, source_target_pairs={{0,2},{2,4},{4,6},{6,8},{8,10},{10,12},{12,14},{14,16},{16,18},{18... | collective-permute-start | bytes 36872 | tf_op jit(solution)/shard_map/ppermute | solution.py:499
  54.0 10.8 %collective-permute-start.4 = (bf16[16,384]{1,0:T(8,128)(2,1)S(1)}, bf16[16,384]{1,0:T(8,128)(2,1)S(1)}, u32[]{:S(2)}, u32[]{:S(2)}) collective-permute-start(bf16[16,384]{1,0:T(8,128)(2,1)S(1)} %get-tuple-element.23), channel_id=1, source_target_pairs={{0,4},{2,6},{4,8},{6,10},{8,12},{10,14},{12,16},{14,18},{16,20},{1... | collective-permute-start | bytes 36872 | tf_op jit(solution)/shard_map/ppermute | solution.py:500
  58.3 6.5 %collective-permute-start.5 = (f32[8,128]{1,0:T(8,128)S(1)}, f32[8,128]{1,0:T(8,128)S(1)}, u32[]{:S(2)}, u32[]{:S(2)}) collective-permute-start(f32[8,128]{1,0:T(8,128)S(1)} %get-tuple-element.24), channel_id=1, source_target_pairs={{0,0},{1,3},{2,2},{3,5},{4,4},{5,7},{6,6},{7,9},{8,8},{9,11},{10,1... | collective-permute-start | bytes 12296 | tf_op jit(solution)/shard_map/ppermute | solution.py:501
  64.9 15.0 %copy-start.1 = (bf16[8,9216]{1,0:T(8,128)(2,1)S(1)}, bf16[8,9216]{1,0:T(8,128)(2,1)}, u32[]{:S(2)}) copy-start(bf16[8,9216]{1,0:T(8,128)(2,1)} %dens.3) | copy-start | bytes 442372

commit v5 on v4

--- a/solution.py
+++ b/solution.py
@@ -10,8 +10,8 @@
 NA = 16
 REACH = 3
 PURIF = 12
-UNROLL = 6
-BATCH = 8
+UNROLL = 12
+BATCH = 16
 FRAG_DEV = 8
 DIM_DEV = 4
 FLAT = NB * NB

time: 81.5 us -> 81.3 us (level)
  no operation moved by 1% of the time
where the time goes in v5:
time: 81.3 us; the launch traced here: 80.8 us
  blocking collectives  31.2 us (38%)
  starting transfers between devices  25.4 us (31%)
  Pallas kernels  15.4 us (19%)
  waiting for transfers between devices  7.92 us (10%)
    all_to_all x2, blocking collectives, exchange(): return lax.all_to_all(value, axis, split_axis=0, concat_axis=0, tiled=True)  31.2 us
    all_to_all x1, starting transfers between devices, exchange(): return lax.all_to_all(value, axis, split_axis=0, concat_axis=0, tiled=True)  11.3 us
    pallas_call x1, Pallas kernels, solve_dimers(): pl.pallas_call(solve_kernel, out_shape=(jax.ShapeDtypeStruct((N_TEAM * 8...  9.33 us
    ppermute x3, starting transfers between devices, per_device(): focks.append(lax.ppermute(packed, FRAG, moves))  4.73 us
    ppermute x1, starting transfers between devices, per_device(): lax.ppermute(next_2, PAIR, [(index, index + 2) for index in range(N_PAIR...  4.45 us
    all_to_all x1, waiting for transfers between devices, exchange(): return lax.all_to_all(value, axis, split_axis=0, concat_axis=0, tiled=True)  4.12 us
    ppermute x1, waiting for transfers between devices, per_device(): energy = lax.ppermute(energy, GRP_FRAG, energy_moves())  3.79 us
    ppermute x1, starting transfers between devices, per_device(): energy = lax.ppermute(energy, GRP_FRAG, energy_moves())  2.66 us
  transfers between devices with their start and end apart: 7, of which 2 were waited for; matrix products, arithmetic and copies ran while one was open for 0% of the time, Pallas kernels for 3%

profile of v5, /device:TPU:1, one launch (start us, length us, event | category | flops | bytes accessed | tf_op | source)
XLA Modules:
  0.0 80.8 jit_solution(15161185326475666243)
XLA Ops:
  0.6 0.0 copy-start.3
  0.6 2.0 %atom_table.1 = (f32[32,8,128]{2,1,0:T(8,128)}, bf16[384,128]{1,0:T(8,128)(2,1)}) custom-call(s32[8]{0:T(128)} %counts.1, bf16[8,9216]{1,0:T(8,128)(2,1)} %dens.3, bf16[8,9216]{1,0:T(8,128)(2,1)} %fock.3, f32[1,128]{1,0:T(1,128)} %bitcast.6, f32[3,128]{1,0:T(4,128)} %coords.1), custom_call_target="tpu_custom_call" | custom-call | tf_op jit(solution)/shard_map/atom_table/pallas_call | solution.py:128
  2.7 0.0 copy-start
  2.7 11.3 %all-to-all-start = ((f32[32,8,128]{2,1,0:T(8,128)}), f32[32,8,128]{2,1,0:T(8,128)S(1)}, u32[]{:S(2)}, u32[]{:S(2)}) async-start(f32[32,8,128]{2,1,0:T(8,128)} %get-tuple-element.16), calls=%async_computation | async-start | bytes 262144 | tf_op jit(solution)/shard_map/all_to_all | solution.py:43
  13.9 0.0 copy-start.4
  13.9 0.0 copy-done.2
  13.9 1.3 %collective-permute-start.2 = (bf16[384,128]{1,0:T(8,128)(2,1)S(1)}, bf16[384,128]{1,0:T(8,128)(2,1)S(1)}, u32[]{:S(2)}, u32[]{:S(2)}) collective-permute-start(bf16[384,128]{1,0:T(8,128)(2,1)S(1)} %copy-done.2), channel_id=1, source_target_pairs={{3,0},{4,1},{5,2},{6,3},{7,4},{8,5},{9,6},{10,7},{11,8},{12,9},{13... | collective-permute-start | bytes 294920 | tf_op jit(solution)/shard_map/ppermute | solution.py:493
  15.2 1.3 %collective-permute-start.1 = (bf16[384,128]{1,0:T(8,128)(2,1)S(1)}, bf16[384,128]{1,0:T(8,128)(2,1)S(1)}, u32[]{:S(2)}, u32[]{:S(2)}) collective-permute-start(bf16[384,128]{1,0:T(8,128)(2,1)S(1)} %copy-done.2), channel_id=1, source_target_pairs={{2,0},{3,1},{4,2},{5,3},{6,4},{7,5},{8,6},{9,7},{10,8},{11,9},{12,... | collective-permute-start | bytes 294920 | tf_op jit(solution)/shard_map/ppermute | solution.py:493
  16.5 2.1 %collective-permute-start = (bf16[384,128]{1,0:T(8,128)(2,1)S(1)}, bf16[384,128]{1,0:T(8,128)(2,1)S(1)}, u32[]{:S(2)}, u32[]{:S(2)}) collective-permute-start(bf16[384,128]{1,0:T(8,128)(2,1)S(1)} %copy-done.2), channel_id=1, source_target_pairs={{1,0},{2,1},{3,2},{4,3},{5,4},{6,5},{7,6},{8,7},{9,8},{10,9},{11,1... | collective-permute-start | bytes 294920 | tf_op jit(solution)/shard_map/ppermute | solution.py:493
  18.7 0.0 copy-done.4
  18.7 0.1 copy.11.pairs
  18.8 4.1 %all-to-all-done.table = f32[32,8,128]{2,1,0:T(8,128)S(1)} async-done(((f32[32,8,128]{2,1,0:T(8,128)}), f32[32,8,128]{2,1,0:T(8,128)S(1)}, u32[]{:S(2)}, u32[]{:S(2)}) %all-to-all-start) | async-done | bytes 131104 | tf_op jit(solution)/shard_map/all_to_all | solution.py:43
  22.9 0.0 copy-done.3
  22.9 0.0 copy-done
  22.9 2.5 %prepare_dimers.1 = (f32[4,192,256]{2,1,0:T(8,128)S(1)}, f32[8,128]{1,0:T(8,128)S(1)}) custom-call(s32[4,2]{1,0:T(4,128)S(1)} %copy.11.pairs, f32[32,8,128]{2,1,0:T(8,128)S(1)} %all-to-all-done.table, bf16[8,9216]{1,0:T(8,128)(2,1)S(1)} %copy-done, bf16[4,9216]{1,0:T(4,128)(2,1)S(1)} %copy-done.3), custom_call_target="tpu_custom_call" | custom-call | tf_op jit(solution)/shard_map/prepare_dimers/pallas_call | solution.py:223
  25.4 0.0 collective-permute-done.2.fock_3
  25.4 0.0 collective-permute-done.1.fock_2
  25.4 0.0 collective-permute-done.fock_1
  25.4 9.3 %solve_dimers.1 = (f32[384,128]{1,0:T(8,128)S(1)}, f32[8,128]{1,0:T(8,128)S(1)}) custom-call(s32[4,2]{1,0:T(4,128)S(1)} %copy.11.pairs, f32[4,192,256]{2,1,0:T(8,128)S(1)} %get-tuple-element.17.fixed, f32[8,128]{1,0:T(8,128)S(1)} %get-tuple-element.18.starts, bf16[384,128]{1,0:T(8,128)(2,1)S(1)} %copy-done.2, ...), custom_call_target="tpu_custom_call" | custom-call | tf_op jit(solution)/shard_map/solve_dimers/pallas_call | solution.py:333
  34.8 16.2 %all_to_all.15.arrived = f32[16,24,128]{2,1,0:T(8,128)S(1)} all-to-all(f32[16,24,128]{2,1,0:T(8,128)S(1)} %bitcast.5), channel_id=1, replica_groups=mesh['grp_0'=2,'grp_1'=4,'frag_0'=2,'frag_1'=8,'frag_2'=2] {'grp_0','grp..., dimensions={0} | all-to-all | bytes 393216 | tf_op jit(solution)/shard_map/all_to_all | solution.py:43
  51.0 0.3 sort_blocks.1
  51.3 2.3 %collective-permute-start.3 = (bf16[16,384]{1,0:T(8,128)(2,1)S(1)}, bf16[16,384]{1,0:T(8,128)(2,1)S(1)}, u32[]{:S(2)}, u32[]{:S(2)}) collective-permute-start(bf16[16,384]{1,0:T(8,128)(2,1)S(1)} %get-tuple-element.22), channel_id=1, source_target_pairs={{0,2},{2,4},{4,6},{6,8},{8,10},{10,12},{12,14},{14,16},{16,18},{18... | collective-permute-start | bytes 36872 | tf_op jit(solution)/shard_map/ppermute | solution.py:499
  53.6 4.4 %collective-permute-start.4 = (bf16[16,384]{1,0:T(8,128)(2,1)S(1)}, bf16[16,384]{1,0:T(8,128)(2,1)S(1)}, u32[]{:S(2)}, u32[]{:S(2)}) collective-permute-start(bf16[16,384]{1,0:T(8,128)(2,1)S(1)} %get-tuple-element.23), channel_id=1, source_target_pairs={{0,4},{2,6},{4,8},{6,10},{8,12},{10,14},{12,16},{14,18},{16,20},{1... | collective-permute-start | bytes 36872 | tf_op jit(solution)/shard_map/ppermute | solution.py:500
  58.1 2.7 %collective-permute-start.5 = (f32[8,128]{1,0:T(8,128)S(1)}, f32[8,128]{1,0:T(8,128)S(1)}, u32[]{:S(2)}, u32[]{:S(2)}) collective-permute-start(f32[8,128]{1,0:T(8,128)S(1)} %get-tuple-element.24), channel_id=1, source_target_pairs={{0,0},{1,3},{2,2},{3,5},{4,4},{5,7},{6,6},{7,9},{8,8},{9,11},{10,1... | collective-permute-start | bytes 12296 | tf_op jit(solution)/shard_map/ppermute | solution.py:501
  60.7 3.8 %collective-permute-done.5.energy = f32[8,128]{1,0:T(8,128)S(1)} collective-permute-done((f32[8,128]{1,0:T(8,128)S(1)}, f32[8,128]{1,0:T(8,128)S(1)}, u32[]{:S(2)}, u32[]{:S(2)}) %collective-permute-start.5) | collective-permute-done | bytes 4128 | tf_op jit(solution)/shard_map/ppermute | solution.py:501
  64.5 0.0 collective-permute-done.3.from_1
  64.5 0.0 collective-permute-done.4.from_2
  64.5 0.1 join_blocks.1
  64.6 0.0 copy-start.1
  64.7 15.0 %all_to_all.16 = f32[16,24,128]{2,1,0:T(8,128)S(1)} all-to-all(f32[16,24,128]{2,1,0:T(8,128)S(1)} %join_blocks.1), channel_id=1, replica_groups=mesh['grp_0'=2,'grp_1'=4,'frag_0'=2,'frag_1'=8,'frag_2'=2] {'grp_0','grp..., dimensions={0} | all-to-all | bytes 393216 | tf_op jit(solution)/shard_map/all_to_all | solution.py:43
  79.7 0.0 copy-done.1
  79.7 1.2 %unpack_blocks.1 = (f32[8,9216]{1,0:T(8,128)}, f32[1]{0:T(128)}, f32[4]{0:T(128)}) custom-call(f32[384,128]{1,0:T(8,128)S(1)} %bitcast.4, bf16[8,9216]{1,0:T(8,128)(2,1)S(1)} %copy-done.1, f32[8,128]{1,0:T(8,128)S(1)} %get-tuple-element.25.energy_rows), custom_call_target="tpu_custom_call" | custom-call | tf_op jit(solution)/shard_map/unpack_blocks/pallas_call | solution.py:458
  (1 shorter events, 0.0 us)
Async XLA Ops:
  0.6 22.3 %copy-start.3 = (bf16[4,9216]{1,0:T(4,128)(2,1)S(1)}, bf16[4,9216]{1,0:T(4,128)(2,1)}, u32[]{:S(2)}) copy-start(bf16[4,9216]{1,0:T(4,128)(2,1)} %coupling.1) | copy-start | bytes 221188
  2.7 20.3 %copy-start = (bf16[8,9216]{1,0:T(8,128)(2,1)S(1)}, bf16[8,9216]{1,0:T(8,128)(2,1)}, u32[]{:S(2)}) copy-start(bf16[8,9216]{1,0:T(8,128)(2,1)} %fock.3) | copy-start | bytes 442372
  2.7 11.3 %copy-start.2 = (bf16[384,128]{1,0:T(8,128)(2,1)S(1)}, bf16[384,128]{1,0:T(8,128)(2,1)}, u32[]{:S(2)}) copy-start(bf16[384,128]{1,0:T(8,128)(2,1)} %get-tuple-element.19.fock_0) | copy-start | bytes 294916
  2.7 20.3 %all-to-all-start = ((f32[32,8,128]{2,1,0:T(8,128)}), f32[32,8,128]{2,1,0:T(8,128)S(1)}, u32[]{:S(2)}, u32[]{:S(2)}) async-start(f32[32,8,128]{2,1,0:T(8,128)} %get-tuple-element.16), calls=%async_computation | async-start | bytes 262144 | tf_op jit(solution)/shard_map/all_to_all | solution.py:43
  13.9 4.8 %copy-start.4 = (s32[4,2]{0,1:T(2,128)S(1)}, s32[4,2]{0,1:T(2,128)}, u32[]{:S(2)}) copy-start(s32[4,2]{0,1:T(2,128)} %param.10) | copy-start | bytes 100
  13.9 11.5 %collective-permute-start.2 = (bf16[384,128]{1,0:T(8,128)(2,1)S(1)}, bf16[384,128]{1,0:T(8,128)(2,1)S(1)}, u32[]{:S(2)}, u32[]{:S(2)}) collective-permute-start(bf16[384,128]{1,0:T(8,128)(2,1)S(1)} %copy-done.2), channel_id=1, source_target_pairs={{3,0},{4,1},{5,2},{6,3},{7,4},{8,5},{9,6},{10,7},{11,8},{12,9},{13... | collective-permute-start | bytes 294920 | tf_op jit(solution)/shard_map/ppermute | solution.py:493
  15.2 10.2 %collective-permute-start.1 = (bf16[384,128]{1,0:T(8,128)(2,1)S(1)}, bf16[384,128]{1,0:T(8,128)(2,1)S(1)}, u32[]{:S(2)}, u32[]{:S(2)}) collective-permute-start(bf16[384,128]{1,0:T(8,128)(2,1)S(1)} %copy-done.2), channel_id=1, source_target_pairs={{2,0},{3,1},{4,2},{5,3},{6,4},{7,5},{8,6},{9,7},{10,8},{11,9},{12,... | collective-permute-start | bytes 294920 | tf_op jit(solution)/shard_map/ppermute | solution.py:493
  16.5 8.9 %collective-permute-start = (bf16[384,128]{1,0:T(8,128)(2,1)S(1)}, bf16[384,128]{1,0:T(8,128)(2,1)S(1)}, u32[]{:S(2)}, u32[]{:S(2)}) collective-permute-start(bf16[384,128]{1,0:T(8,128)(2,1)S(1)} %copy-done.2), channel_id=1, source_target_pairs={{1,0},{2,1},{3,2},{4,3},{5,4},{6,5},{7,6},{8,7},{9,8},{10,9},{11,1... | collective-permute-start | bytes 294920 | tf_op jit(solution)/shard_map/ppermute | solution.py:493
  51.3 13.2 %collective-permute-start.3 = (bf16[16,384]{1,0:T(8,128)(2,1)S(1)}, bf16[16,384]{1,0:T(8,128)(2,1)S(1)}, u32[]{:S(2)}, u32[]{:S(2)}) collective-permute-start(bf16[16,384]{1,0:T(8,128)(2,1)S(1)} %get-tuple-element.22), channel_id=1, source_target_pairs={{0,2},{2,4},{4,6},{6,8},{8,10},{10,12},{12,14},{14,16},{16,18},{18... | collective-permute-start | bytes 36872 | tf_op jit(solution)/shard_map/ppermute | solution.py:499
  53.6 10.9 %collective-permute-start.4 = (bf16[16,384]{1,0:T(8,128)(2,1)S(1)}, bf16[16,384]{1,0:T(8,128)(2,1)S(1)}, u32[]{:S(2)}, u32[]{:S(2)}) collective-permute-start(bf16[16,384]{1,0:T(8,128)(2,1)S(1)} %get-tuple-element.23), channel_id=1, source_target_pairs={{0,4},{2,6},{4,8},{6,10},{8,12},{10,14},{12,16},{14,18},{16,20},{1... | collective-permute-start | bytes 36872 | tf_op jit(solution)/shard_map/ppermute | solution.py:500
  58.1 6.5 %collective-permute-start.5 = (f32[8,128]{1,0:T(8,128)S(1)}, f32[8,128]{1,0:T(8,128)S(1)}, u32[]{:S(2)}, u32[]{:S(2)}) collective-permute-start(f32[8,128]{1,0:T(8,128)S(1)} %get-tuple-element.24), channel_id=1, source_target_pairs={{0,0},{1,3},{2,2},{3,5},{4,4},{5,7},{6,6},{7,9},{8,8},{9,11},{10,1... | collective-permute-start | bytes 12296 | tf_op jit(solution)/shard_map/ppermute | solution.py:501
  64.6 15.0 %copy-start.1 = (bf16[8,9216]{1,0:T(8,128)(2,1)S(1)}, bf16[8,9216]{1,0:T(8,128)(2,1)}, u32[]{:S(2)}) copy-start(bf16[8,9216]{1,0:T(8,128)(2,1)} %dens.3) | copy-start | bytes 442372

commit v6 on v5

--- a/solution.py
+++ b/solution.py
@@ -11,7 +11,7 @@
 REACH = 3
 PURIF = 12
 UNROLL = 12
-BATCH = 16
+BATCH = 32
 FRAG_DEV = 8
 DIM_DEV = 4
 FLAT = NB * NB

time: 81.3 us -> 81.3 us (level)
  no operation moved by 1% of the time
where the time goes in v6:
time: 81.3 us; the launch traced here: 80.8 us
  blocking collectives  31.2 us (38%)
  starting transfers between devices  25.6 us (31%)
  Pallas kernels  15.2 us (19%)
  waiting for transfers between devices  7.92 us (10%)
    all_to_all x2, blocking collectives, exchange(): return lax.all_to_all(value, axis, split_axis=0, concat_axis=0, tiled=True)  31.2 us
    all_to_all x1, starting transfers between devices, exchange(): return lax.all_to_all(value, axis, split_axis=0, concat_axis=0, tiled=True)  11.3 us
    pallas_call x1, Pallas kernels, solve_dimers(): pl.pallas_call(solve_kernel, out_shape=(jax.ShapeDtypeStruct((N_TEAM * 8...  9.33 us
    ppermute x3, starting transfers between devices, per_device(): focks.append(lax.ppermute(packed, FRAG, moves))  4.73 us
    ppermute x1, starting transfers between devices, per_device(): lax.ppermute(next_2, PAIR, [(index, index + 2) for index in range(N_PAIR...  4.66 us
    all_to_all x1, waiting for transfers between devices, exchange(): return lax.all_to_all(value, axis, split_axis=0, concat_axis=0, tiled=True)  4.12 us
    ppermute x1, waiting for transfers between devices, per_device(): energy = lax.ppermute(energy, GRP_FRAG, energy_moves())  3.79 us
    ppermute x1, starting transfers between devices, per_device(): energy = lax.ppermute(energy, GRP_FRAG, energy_moves())  2.66 us
  transfers between devices with their start and end apart: 7, of which 2 were waited for; matrix products, arithmetic and copies ran while one was open for 0% of the time, Pallas kernels for 3%

profile of v6, /device:TPU:1, one launch (start us, length us, event | category | flops | bytes accessed | tf_op | source)
XLA Modules:
  0.0 80.8 jit_solution(5023000571396498392)
XLA Ops:
  0.6 0.0 copy-start.3
  0.6 2.0 %atom_table.1 = (f32[32,8,128]{2,1,0:T(8,128)}, bf16[384,128]{1,0:T(8,128)(2,1)}) custom-call(s32[8]{0:T(128)} %counts.1, bf16[8,9216]{1,0:T(8,128)(2,1)} %dens.3, bf16[8,9216]{1,0:T(8,128)(2,1)} %fock.3, f32[1,128]{1,0:T(1,128)} %bitcast.6, f32[3,128]{1,0:T(4,128)} %coords.1), custom_call_target="tpu_custom_call" | custom-call | tf_op jit(solution)/shard_map/atom_table/pallas_call | solution.py:128
  2.7 0.0 copy-start
  2.7 11.3 %all-to-all-start = ((f32[32,8,128]{2,1,0:T(8,128)}), f32[32,8,128]{2,1,0:T(8,128)S(1)}, u32[]{:S(2)}, u32[]{:S(2)}) async-start(f32[32,8,128]{2,1,0:T(8,128)} %get-tuple-element.16), calls=%async_computation | async-start | bytes 262144 | tf_op jit(solution)/shard_map/all_to_all | solution.py:43
  13.9 0.0 copy-start.4
  13.9 0.0 copy-done.2
  13.9 1.3 %collective-permute-start.2 = (bf16[384,128]{1,0:T(8,128)(2,1)S(1)}, bf16[384,128]{1,0:T(8,128)(2,1)S(1)}, u32[]{:S(2)}, u32[]{:S(2)}) collective-permute-start(bf16[384,128]{1,0:T(8,128)(2,1)S(1)} %copy-done.2), channel_id=1, source_target_pairs={{3,0},{4,1},{5,2},{6,3},{7,4},{8,5},{9,6},{10,7},{11,8},{12,9},{13... | collective-permute-start | bytes 294920 | tf_op jit(solution)/shard_map/ppermute | solution.py:493
  15.2 1.3 %collective-permute-start.1 = (bf16[384,128]{1,0:T(8,128)(2,1)S(1)}, bf16[384,128]{1,0:T(8,128)(2,1)S(1)}, u32[]{:S(2)}, u32[]{:S(2)}) collective-permute-start(bf16[384,128]{1,0:T(8,128)(2,1)S(1)} %copy-done.2), channel_id=1, source_target_pairs={{2,0},{3,1},{4,2},{5,3},{6,4},{7,5},{8,6},{9,7},{10,8},{11,9},{12,... | collective-permute-start | bytes 294920 | tf_op jit(solution)/shard_map/ppermute | solution.py:493
  16.5 2.1 %collective-permute-start = (bf16[384,128]{1,0:T(8,128)(2,1)S(1)}, bf16[384,128]{1,0:T(8,128)(2,1)S(1)}, u32[]{:S(2)}, u32[]{:S(2)}) collective-permute-start(bf16[384,128]{1,0:T(8,128)(2,1)S(1)} %copy-done.2), channel_id=1, source_target_pairs={{1,0},{2,1},{3,2},{4,3},{5,4},{6,5},{7,6},{8,7},{9,8},{10,9},{11,1... | collective-permute-start | bytes 294920 | tf_op jit(solution)/shard_map/ppermute | solution.py:493
  18.7 0.0 copy-done.4
  18.7 0.1 copy.11.pairs
  18.8 4.1 %all-to-all-done.table = f32[32,8,128]{2,1,0:T(8,128)S(1)} async-done(((f32[32,8,128]{2,1,0:T(8,128)}), f32[32,8,128]{2,1,0:T(8,128)S(1)}, u32[]{:S(2)}, u32[]{:S(2)}) %all-to-all-start) | async-done | bytes 131104 | tf_op jit(solution)/shard_map/all_to_all | solution.py:43
  22.9 0.0 copy-done.3
  22.9 0.0 copy-done
  22.9 2.3 %prepare_dimers.1 = (f32[4,192,256]{2,1,0:T(8,128)S(1)}, f32[8,128]{1,0:T(8,128)S(1)}) custom-call(s32[4,2]{1,0:T(4,128)S(1)} %copy.11.pairs, f32[32,8,128]{2,1,0:T(8,128)S(1)} %all-to-all-done.table, bf16[8,9216]{1,0:T(8,128)(2,1)S(1)} %copy-done, bf16[4,9216]{1,0:T(4,128)(2,1)S(1)} %copy-done.3), custom_call_target="tpu_custom_call" | custom-call | tf_op jit(solution)/shard_map/prepare_dimers/pallas_call | solution.py:223
  25.2 0.0 collective-permute-done.2.fock_3
  25.2 0.0 collective-permute-done.1.fock_2
  25.2 0.0 collective-permute-done.fock_1
  25.2 9.3 %solve_dimers.1 = (f32[384,128]{1,0:T(8,128)S(1)}, f32[8,128]{1,0:T(8,128)S(1)}) custom-call(s32[4,2]{1,0:T(4,128)S(1)} %copy.11.pairs, f32[4,192,256]{2,1,0:T(8,128)S(1)} %get-tuple-element.17.fixed, f32[8,128]{1,0:T(8,128)S(1)} %get-tuple-element.18.starts, bf16[384,128]{1,0:T(8,128)(2,1)S(1)} %copy-done.2, ...), custom_call_target="tpu_custom_call" | custom-call | tf_op jit(solution)/shard_map/solve_dimers/pallas_call | solution.py:333
  34.6 16.2 %all_to_all.15.arrived = f32[16,24,128]{2,1,0:T(8,128)S(1)} all-to-all(f32[16,24,128]{2,1,0:T(8,128)S(1)} %bitcast.5), channel_id=1, replica_groups=mesh['grp_0'=2,'grp_1'=4,'frag_0'=2,'frag_1'=8,'frag_2'=2] {'grp_0','grp..., dimensions={0} | all-to-all | bytes 393216 | tf_op jit(solution)/shard_map/all_to_all | solution.py:43
  50.8 0.3 sort_blocks.1
  51.1 2.3 %collective-permute-start.3 = (bf16[16,384]{1,0:T(8,128)(2,1)S(1)}, bf16[16,384]{1,0:T(8,128)(2,1)S(1)}, u32[]{:S(2)}, u32[]{:S(2)}) collective-permute-start(bf16[16,384]{1,0:T(8,128)(2,1)S(1)} %get-tuple-element.22), channel_id=1, source_target_pairs={{0,2},{2,4},{4,6},{6,8},{8,10},{10,12},{12,14},{14,16},{16,18},{18... | collective-permute-start | bytes 36872 | tf_op jit(solution)/shard_map/ppermute | solution.py:499
  53.4 4.7 %collective-permute-start.4 = (bf16[16,384]{1,0:T(8,128)(2,1)S(1)}, bf16[16,384]{1,0:T(8,128)(2,1)S(1)}, u32[]{:S(2)}, u32[]{:S(2)}) collective-permute-start(bf16[16,384]{1,0:T(8,128)(2,1)S(1)} %get-tuple-element.23), channel_id=1, source_target_pairs={{0,4},{2,6},{4,8},{6,10},{8,12},{10,14},{12,16},{14,18},{16,20},{1... | collective-permute-start | bytes 36872 | tf_op jit(solution)/shard_map/ppermute | solution.py:500
  58.1 2.7 %collective-permute-start.5 = (f32[8,128]{1,0:T(8,128)S(1)}, f32[8,128]{1,0:T(8,128)S(1)}, u32[]{:S(2)}, u32[]{:S(2)}) collective-permute-start(f32[8,128]{1,0:T(8,128)S(1)} %get-tuple-element.24), channel_id=1, source_target_pairs={{0,0},{1,3},{2,2},{3,5},{4,4},{5,7},{6,6},{7,9},{8,8},{9,11},{10,1... | collective-permute-start | bytes 12296 | tf_op jit(solution)/shard_map/ppermute | solution.py:501
  60.7 3.8 %collective-permute-done.5.energy = f32[8,128]{1,0:T(8,128)S(1)} collective-permute-done((f32[8,128]{1,0:T(8,128)S(1)}, f32[8,128]{1,0:T(8,128)S(1)}, u32[]{:S(2)}, u32[]{:S(2)}) %collective-permute-start.5) | collective-permute-done | bytes 4128 | tf_op jit(solution)/shard_map/ppermute | solution.py:501
  64.5 0.0 collective-permute-done.3.from_1
  64.5 0.0 collective-permute-done.4.from_2
  64.5 0.1 join_blocks.1
  64.6 0.0 copy-start.1
  64.7 15.0 %all_to_all.16 = f32[16,24,128]{2,1,0:T(8,128)S(1)} all-to-all(f32[16,24,128]{2,1,0:T(8,128)S(1)} %join_blocks.1), channel_id=1, replica_groups=mesh['grp_0'=2,'grp_1'=4,'frag_0'=2,'frag_1'=8,'frag_2'=2] {'grp_0','grp..., dimensions={0} | all-to-all | bytes 393216 | tf_op jit(solution)/shard_map/all_to_all | solution.py:43
  79.7 0.0 copy-done.1
  79.7 1.2 %unpack_blocks.1 = (f32[8,9216]{1,0:T(8,128)}, f32[1]{0:T(128)}, f32[4]{0:T(128)}) custom-call(f32[384,128]{1,0:T(8,128)S(1)} %bitcast.4, bf16[8,9216]{1,0:T(8,128)(2,1)S(1)} %copy-done.1, f32[8,128]{1,0:T(8,128)S(1)} %get-tuple-element.25.energy_rows), custom_call_target="tpu_custom_call" | custom-call | tf_op jit(solution)/shard_map/unpack_blocks/pallas_call | solution.py:458
  (1 shorter events, 0.0 us)
Async XLA Ops:
  0.6 22.3 %copy-start.3 = (bf16[4,9216]{1,0:T(4,128)(2,1)S(1)}, bf16[4,9216]{1,0:T(4,128)(2,1)}, u32[]{:S(2)}) copy-start(bf16[4,9216]{1,0:T(4,128)(2,1)} %coupling.1) | copy-start | bytes 221188
  2.7 20.3 %copy-start = (bf16[8,9216]{1,0:T(8,128)(2,1)S(1)}, bf16[8,9216]{1,0:T(8,128)(2,1)}, u32[]{:S(2)}) copy-start(bf16[8,9216]{1,0:T(8,128)(2,1)} %fock.3) | copy-start | bytes 442372
  2.7 11.3 %copy-start.2 = (bf16[384,128]{1,0:T(8,128)(2,1)S(1)}, bf16[384,128]{1,0:T(8,128)(2,1)}, u32[]{:S(2)}) copy-start(bf16[384,128]{1,0:T(8,128)(2,1)} %get-tuple-element.19.fock_0) | copy-start | bytes 294916
  2.7 20.3 %all-to-all-start = ((f32[32,8,128]{2,1,0:T(8,128)}), f32[32,8,128]{2,1,0:T(8,128)S(1)}, u32[]{:S(2)}, u32[]{:S(2)}) async-start(f32[32,8,128]{2,1,0:T(8,128)} %get-tuple-element.16), calls=%async_computation | async-start | bytes 262144 | tf_op jit(solution)/shard_map/all_to_all | solution.py:43
  13.9 4.8 %copy-start.4 = (s32[4,2]{0,1:T(2,128)S(1)}, s32[4,2]{0,1:T(2,128)}, u32[]{:S(2)}) copy-start(s32[4,2]{0,1:T(2,128)} %param.10) | copy-start | bytes 100
  13.9 11.3 %collective-permute-start.2 = (bf16[384,128]{1,0:T(8,128)(2,1)S(1)}, bf16[384,128]{1,0:T(8,128)(2,1)S(1)}, u32[]{:S(2)}, u32[]{:S(2)}) collective-permute-start(bf16[384,128]{1,0:T(8,128)(2,1)S(1)} %copy-done.2), channel_id=1, source_target_pairs={{3,0},{4,1},{5,2},{6,3},{7,4},{8,5},{9,6},{10,7},{11,8},{12,9},{13... | collective-permute-start | bytes 294920 | tf_op jit(solution)/shard_map/ppermute | solution.py:493
  15.2 10.0 %collective-permute-start.1 = (bf16[384,128]{1,0:T(8,128)(2,1)S(1)}, bf16[384,128]{1,0:T(8,128)(2,1)S(1)}, u32[]{:S(2)}, u32[]{:S(2)}) collective-permute-start(bf16[384,128]{1,0:T(8,128)(2,1)S(1)} %copy-done.2), channel_id=1, source_target_pairs={{2,0},{3,1},{4,2},{5,3},{6,4},{7,5},{8,6},{9,7},{10,8},{11,9},{12,... | collective-permute-start | bytes 294920 | tf_op jit(solution)/shard_map/ppermute | solution.py:493
  16.5 8.7 %collective-permute-start = (bf16[384,128]{1,0:T(8,128)(2,1)S(1)}, bf16[384,128]{1,0:T(8,128)(2,1)S(1)}, u32[]{:S(2)}, u32[]{:S(2)}) collective-permute-start(bf16[384,128]{1,0:T(8,128)(2,1)S(1)} %copy-done.2), channel_id=1, source_target_pairs={{1,0},{2,1},{3,2},{4,3},{5,4},{6,5},{7,6},{8,7},{9,8},{10,9},{11,1... | collective-permute-start | bytes 294920 | tf_op jit(solution)/shard_map/ppermute | solution.py:493
  51.1 13.4 %collective-permute-start.3 = (bf16[16,384]{1,0:T(8,128)(2,1)S(1)}, bf16[16,384]{1,0:T(8,128)(2,1)S(1)}, u32[]{:S(2)}, u32[]{:S(2)}) collective-permute-start(bf16[16,384]{1,0:T(8,128)(2,1)S(1)} %get-tuple-element.22), channel_id=1, source_target_pairs={{0,2},{2,4},{4,6},{6,8},{8,10},{10,12},{12,14},{14,16},{16,18},{18... | collective-permute-start | bytes 36872 | tf_op jit(solution)/shard_map/ppermute | solution.py:499
  53.4 11.1 %collective-permute-start.4 = (bf16[16,384]{1,0:T(8,128)(2,1)S(1)}, bf16[16,384]{1,0:T(8,128)(2,1)S(1)}, u32[]{:S(2)}, u32[]{:S(2)}) collective-permute-start(bf16[16,384]{1,0:T(8,128)(2,1)S(1)} %get-tuple-element.23), channel_id=1, source_target_pairs={{0,4},{2,6},{4,8},{6,10},{8,12},{10,14},{12,16},{14,18},{16,20},{1... | collective-permute-start | bytes 36872 | tf_op jit(solution)/shard_map/ppermute | solution.py:500
  58.1 6.5 %collective-permute-start.5 = (f32[8,128]{1,0:T(8,128)S(1)}, f32[8,128]{1,0:T(8,128)S(1)}, u32[]{:S(2)}, u32[]{:S(2)}) collective-permute-start(f32[8,128]{1,0:T(8,128)S(1)} %get-tuple-element.24), channel_id=1, source_target_pairs={{0,0},{1,3},{2,2},{3,5},{4,4},{5,7},{6,6},{7,9},{8,8},{9,11},{10,1... | collective-permute-start | bytes 12296 | tf_op jit(solution)/shard_map/ppermute | solution.py:501
  64.6 15.0 %copy-start.1 = (bf16[8,9216]{1,0:T(8,128)(2,1)S(1)}, bf16[8,9216]{1,0:T(8,128)(2,1)}, u32[]{:S(2)}) copy-start(bf16[8,9216]{1,0:T(8,128)(2,1)} %dens.3) | copy-start | bytes 442372
